TPU v7x, 256 devices: a whole 4x4x8 slice. The times are simulated.
256 devices in a mesh: gx: 16 (over y, x), gy: 8 (over z), gz: 2 (over core).
Axes of the slice: x: 4, y: 4, z: 8, core: 2. Of those that a mesh axis runs over, the one named last changes fastest.
Arguments:
- estimate: float32 [16, 1024, 1024], P('gz', 'gx', 'gy'), may hold values from 0.25 to 4
- view_data: float32 [16, 1024, 1024], P('gz', 'gx', 'gy'), may hold values from 0.25 to 4
- psf_stack: float32 [6, 31, 31, 31], replicated, may hold values from 0.01 to 1.53, as said below
- view_index: int32 [1], replicated, may hold values from 0 to 5
Outputs:
- updated_estimate: float32 [16, 1024, 1024], P('gz', 'gx', 'gy')
- level_one: float32 [8, 512, 512], P('gz', 'gx', 'gy')
- level_two: float32 [4, 256, 256], P('gz', 'gx', 'gy')
- level_three: float32 [2, 128, 128], P('gz', 'gx', 'gy')
- level_four: float32 [1, 64, 64], P(None, 'gx', 'gy')
- level_five: float32 [1, 32, 32], replicated
Inputs may be any that keep to these rules, and one draw needn't show every extreme that they name: `psf_stack`: every entry of every view's point spread function is positive.
All inputs are finite; a program needn't handle non-finite values.
Results may differ from a plain program's by a relative error of at most 0.000075.
Values sent between devices are 32-bit elements; how exact they have to be, the bound alone decides.
A program may use at most 128 MiB of HBM per device.

v0:
```python
import functools

import jax
import jax.numpy as jnp
import numpy as np
from jax import lax
from jax.experimental import pallas as pl
from jax.experimental.pallas import tpu as pltpu
from jax.sharding import PartitionSpec as P

MESH = pl.DeviceIdType.MESH
HALO = 15
EDGE = 16
ROWS, COLUMNS = 64, 128
LX, LY = ROWS + 2 * EDGE, COLUMNS + 2 * EDGE
HALF = LY // 2 + 1
TAPS = 2 * HALO + 1
BF16, F32 = jnp.bfloat16, jnp.float32


def parts_of(table):
    table = np.asarray(table, np.float64)
    high = table.astype(np.float32).astype(BF16)
    low = (table - high.astype(np.float64)).astype(np.float32).astype(BF16)
    return high, low


def stacked(table):
    high, low = parts_of(table)
    return np.concatenate([high, low, high], axis=0)


def beside(table):
    high, low = parts_of(table)
    return np.concatenate([high, high, low], axis=1)


def column_table(positions):
    angle = 2.0 * np.pi / LY * np.outer(positions, np.arange(HALF))
    table = np.zeros((len(positions), 256))
    table[:, :HALF] = np.cos(angle)
    table[:, 128 : 128 + HALF] = -np.sin(angle)
    return table


def row_table(positions):
    angle = 2.0 * np.pi / LX * np.outer(np.arange(LX), positions)
    c, s = np.cos(angle), np.sin(angle)
    return np.block([[c, s], [-s, c]])


def tables():
    inner = column_table(EDGE + np.arange(COLUMNS))
    left = column_table(np.arange(EDGE))
    right = column_table(LY - EDGE + np.arange(EDGE))
    first = stacked(np.concatenate([inner] + [left, right] * 4))
    second = stacked(np.concatenate([inner] + [right, left] * 4))
    rows = beside(row_table(np.arange(LX)))
    angle = 2.0 * np.pi / LX * np.outer(EDGE + np.arange(ROWS), np.arange(LX))
    c, s = np.cos(angle), np.sin(angle)
    rows_back = beside(np.block([[c, -s], [s, c]]))
    angle = 2.0 * np.pi / LY * np.outer(np.arange(HALF), EDGE + np.arange(COLUMNS))
    weight = np.where(np.isin(np.arange(HALF), (0, LY // 2)), 1.0, 2.0)[:, None] / (LX * LY)
    back = np.zeros((256, COLUMNS))
    back[:HALF] = weight * np.cos(angle)
    back[128 : 128 + HALF] = -weight * np.sin(angle)
    columns_back = stacked(back)
    taps = column_table(np.concatenate([np.arange(TAPS) - HALO, [0]]))
    taps[TAPS] = 0.0
    tap_columns = np.concatenate([stacked(taps), np.zeros((32, 256), BF16)], axis=0)
    tap_rows_table = row_table(np.concatenate([np.arange(TAPS) - HALO, [0]]))
    tap_rows_table[:, TAPS] = 0.0
    tap_rows_table[:, 32 + TAPS] = 0.0
    tap_rows = beside(tap_rows_table)
    pools = np.zeros((128, 512), np.float32)
    for level in range(4):
        step = 2 ** (level + 1)
        for column in range(COLUMNS):
            pools[column, 128 * level + column // step] = 1.0 / step
    pools = np.concatenate([pools] * 3, axis=0).astype(BF16)
    return first, second, rows, rows_back, columns_back, tap_columns, tap_rows, pools


def two(x):
    high = x.astype(BF16)
    return high, (x - high.astype(F32)).astype(BF16)


def dot(a, b):
    return jnp.dot(a, b, preferred_element_type=F32)


def left_triple(x):
    high, low = two(x)
    return jnp.concatenate([high, high, low], axis=1)


def right_triple(x):
    high, low = two(x)
    return jnp.concatenate([high, low, high], axis=0)


def exact_triple(x):
    high = x.astype(BF16)
    rest = x - high.astype(F32)
    middle = rest.astype(BF16)
    low = (rest - middle.astype(F32)).astype(BF16)
    return jnp.concatenate([high, middle, low], axis=1)


def body(
    nx,
    ny,
    index_ref,
    est_ref,
    view_ref,
    psf_hbm,
    first_ref,
    second_ref,
    rows_ref,
    rows_back_ref,
    columns_back_ref,
    tap_columns_ref,
    tap_rows_ref,
    pools_ref,
    updated_ref,
    one_ref,
    two_ref,
    three_ref,
    four_ref,
    five_ref,
    psf_ref,
    taps_ref,
    tap_half_ref,
    kernel_ref,
    ratio_ref,
    edge_rows,
    edge_columns,
    packed,
    own_ref,
    other_ref,
    product_ref,
    pool_a,
    pool_b,
    pool_c,
    pool_d,
    plane_ref,
    tile_ref,
    strips_ref,
    local_sem,
    send_sem,
    recv_sem,
    part_send,
    part_recv,
    ring_send,
    ring_recv,
):
    gx, gy, gz = lax.axis_index("gx"), lax.axis_index("gy"), lax.axis_index("gz")

    def device(dx, dy, dz=0):
        return {
            "gx": lax.rem(gx + dx + nx, nx),
            "gy": lax.rem(gy + dy + ny, ny),
            "gz": lax.rem(gz + dz, 2),
        }

    fetch = pltpu.make_async_copy(psf_hbm, psf_ref, local_sem)
    fetch.start()

    peers = [(dx, dy, 0) for dx in (-1, 0, 1) for dy in (-1, 0, 1) if (dx, dy) != (0, 0)]
    peers.append((0, 0, 1))
    peers += [(0, k, 0) for k in range(2, ny - 1)]
    peers += [(k, 0, 0) for k in range(2, nx - 1)]
    barrier = pltpu.get_barrier_semaphore()
    for peer in peers:
        pl.semaphore_signal(barrier, inc=1, device_id=device(*peer), device_id_type=MESH)

    def pack(source, turn):
        lane = lax.broadcasted_iota(jnp.int32, (ROWS, 128), 1)
        to_right = jnp.zeros((ROWS, 128), F32)
        to_left = jnp.zeros((ROWS, 128), F32)
        for z in range(8):
            base = (z % 4) * 32
            low, high = (base, base + EDGE) if z < 4 else (base + EDGE, base)
            plane = source[z]
            shift = (low - (COLUMNS - EDGE)) % 128
            rolled = pltpu.roll(plane, shift, 1) if shift else plane
            to_right = jnp.where((lane >= low) & (lane < low + EDGE), rolled, to_right)
            rolled = pltpu.roll(plane, high, 1) if high else plane
            to_left = jnp.where((lane >= high) & (lane < high + EDGE), rolled, to_left)
        packed[turn, 0] = to_right
        packed[turn, 1] = to_left

    middle, top, bottom = pl.ds(EDGE, ROWS), pl.ds(0, EDGE), pl.ds(EDGE + ROWS, EDGE)
    head, tail = pl.ds(0, EDGE), pl.ds(ROWS - EDGE, EDGE)

    def halo_copies(source, turn):
        def copy(src, dst, at, dx, dy):
            return pltpu.make_async_remote_copy(
                src_ref=src,
                dst_ref=dst,
                send_sem=send_sem.at[turn, at],
                recv_sem=recv_sem.at[turn, at],
                device_id=device(dx, dy),
                device_id_type=MESH,
            )

        right, left = packed.at[turn, 0], packed.at[turn, 1]
        from_left, from_right = edge_columns.at[turn, 0], edge_columns.at[turn, 1]
        return [
            copy(source.at[:, tail, :], edge_rows.at[turn, 0], 0, 1, 0),
            copy(source.at[:, head, :], edge_rows.at[turn, 1], 1, -1, 0),
            copy(right.at[tail, :], from_left.at[top, :], 2, 1, 1),
            copy(right.at[head, :], from_left.at[bottom, :], 3, -1, 1),
            copy(left.at[tail, :], from_right.at[top, :], 4, 1, -1),
            copy(left.at[head, :], from_right.at[bottom, :], 5, -1, -1),
            copy(right, from_left.at[middle, :], 6, 0, 1),
            copy(left, from_right.at[middle, :], 7, 0, -1),
        ]

    def clear_borders(turn):
        @pl.when(gx == 0)
        def _():
            edge_rows[turn, 0] = jnp.zeros((8, EDGE, 128), F32)
            for side in (0, 1):
                edge_columns[turn, side, top, :] = jnp.zeros((EDGE, 128), F32)

        @pl.when(gx == nx - 1)
        def _():
            edge_rows[turn, 1] = jnp.zeros((8, EDGE, 128), F32)
            for side in (0, 1):
                edge_columns[turn, side, bottom, :] = jnp.zeros((EDGE, 128), F32)

        @pl.when(gy == 0)
        def _():
            edge_columns[turn, 0] = jnp.zeros((LX, 128), F32)

        @pl.when(gy == ny - 1)
        def _():
            edge_columns[turn, 1] = jnp.zeros((LX, 128), F32)

    def partner_copy(turn, z):
        return pltpu.make_async_remote_copy(
            src_ref=own_ref.at[turn, z],
            dst_ref=other_ref.at[turn, z],
            send_sem=part_send.at[turn, z],
            recv_sem=part_recv.at[turn, z],
            device_id=device(0, 0, 1),
            device_id_type=MESH,
        )

    def forward(source, turn):
        lane = lax.broadcasted_iota(jnp.int32, (LX, 128), 1)
        even = (lane & EDGE) == 0
        left, right = edge_columns[turn, 0], edge_columns[turn, 1]
        for group, table in ((0, first_ref), (1, second_ref)):
            mixed = jnp.where(even, left, right) if group == 0 else jnp.where(even, right, left)
            rows = []
            for j in range(4):
                z = 4 * group + j
                plane = jnp.concatenate(
                    [edge_rows[turn, 0, z], source[z], edge_rows[turn, 1, z]], axis=0
                )
                side = jnp.where((lane >= 32 * j) & (lane < 32 * j + 32), mixed, 0.0)
                rows.append(jnp.concatenate([plane, side], axis=1))
            half = dot(left_triple(jnp.concatenate(rows, axis=0)), table[...])
            for pair in (0, 1):
                a = half[192 * pair : 192 * pair + 96]
                b = half[192 * pair + 96 : 192 * pair + 192]
                joint = jnp.concatenate(
                    [
                        jnp.concatenate([a[:, :128], b[:, :128]], axis=1),
                        jnp.concatenate([a[:, 128:], b[:, 128:]], axis=1),
                    ],
                    axis=0,
                )
                full = dot(rows_ref[...], right_triple(joint))
                z = 4 * group + 2 * pair
                own_ref[turn, z] = full[:, :128]
                own_ref[turn, z + 1] = full[:, 128:]
                partner_copy(turn, z).start()
                partner_copy(turn, z + 1).start()

    def depth(x_ref, turn, base, mirrored, adding):
        def block(step, carry):
            at = pl.multiple_of(step * 8, 8)
            re, im = pl.ds(at, 8), pl.ds(pl.multiple_of(at + LX, 8), 8)
            xr = [x_ref[turn, z, re, :] for z in range(8)]
            xi = [x_ref[turn, z, im, :] for z in range(8)]
            if adding:
                yr = [product_ref[z, re, :] for z in range(8)]
                yi = [product_ref[z, im, :] for z in range(8)]
            else:
                yr, yi = [None] * 8, [None] * 8
            for d in range(-7, 8):
                kr, ki = kernel_ref[base + d, re, :], kernel_ref[base + d, im, :]
                for out in range(8):
                    z = out + d if mirrored else out - d
                    if not 0 <= z < 8:
                        continue
                    if mirrored:
                        r = kr * xr[z] + ki * xi[z]
                        i = kr * xi[z] - ki * xr[z]
                    else:
                        r = kr * xr[z] - ki * xi[z]
                        i = kr * xi[z] + ki * xr[z]
                    yr[out] = r if yr[out] is None else yr[out] + r
                    yi[out] = i if yi[out] is None else yi[out] + i
            for z in range(8):
                product_ref[z, re, :] = yr[z]
                product_ref[z, im, :] = yi[z]
            return carry

        lax.fori_loop(0, LX // 8, block, 0)

    def inverse(group):
        rows = []
        for pair in (0, 1):
            z = 4 * group + 2 * pair
            joint = jnp.concatenate([product_ref[z], product_ref[z + 1]], axis=1)
            half = dot(rows_back_ref[...], right_triple(joint))
            for b in (0, 1):
                lanes = slice(128 * b, 128 * b + 128)
                rows.append(jnp.concatenate([half[:ROWS, lanes], half[ROWS:, lanes]], axis=1))
        full = dot(left_triple(jnp.concatenate(rows, axis=0)), columns_back_ref[...])
        return full.reshape(4, ROWS, COLUMNS)

    def convolve(source, turn, mirrored):
        forward(source, turn)
        depth(own_ref, turn, HALO, mirrored, False)
        for z in range(8):
            partner_copy(turn, z).wait_recv()
        base = HALO + 8 - 16 * gz if mirrored else HALO - 8 + 16 * gz
        depth(other_ref, turn, base, mirrored, True)

    def spectrum():
        fetch.wait()
        view = index_ref[0]
        taps_ref[...] = jnp.zeros((32, 32, 128), F32)

        def load(z, total):
            values = psf_ref[view, z]
            taps_ref[z, 0:TAPS, 0:TAPS] = values
            return total

        lax.fori_loop(0, TAPS, load, 0)
        total = jnp.sum(jnp.sum(taps_ref[...], axis=0), axis=(0, 1), keepdims=True)
        scale = 1.0 / total

        def columns(step, carry):
            x = taps_ref[pl.ds(step * 8, 8)].reshape(256, 128) * scale
            high = x.astype(BF16).astype(F32)
            low = x - high
            joint = high + pltpu.roll(high, 32, 1) + pltpu.roll(low, 64, 1)
            tap_half_ref[pl.ds(step * 8, 8)] = dot(joint.astype(BF16), tap_columns_ref[...]).reshape(
                8, 32, 256
            )
            return carry

        lax.fori_loop(0, 4, columns, 0)

        def rows(step, carry):
            a, b = tap_half_ref[2 * step], tap_half_ref[2 * step + 1]
            joint = jnp.concatenate(
                [
                    jnp.concatenate([a[:, :128], b[:, :128]], axis=1),
                    jnp.concatenate([a[:, 128:], b[:, 128:]], axis=1),
                ],
                axis=0,
            )
            full = dot(tap_rows_ref[...], right_triple(joint))
            kernel_ref[2 * step] = full[:, :128]
            kernel_ref[2 * step + 1] = full[:, 128:]
            return carry

        lax.fori_loop(0, 16, rows, 0)

    pack(est_ref, 0)
    pl.semaphore_wait(barrier, len(peers))
    copies = halo_copies(est_ref, 0)
    for copy in copies:
        copy.start()
    spectrum()
    for copy in copies:
        copy.wait_recv()
    clear_borders(0)
    convolve(est_ref, 0, False)
    for group in (0, 1):
        at = pl.ds(4 * group, 4)
        ratio_ref[at] = view_ref[at] / inverse(group)

    pack(ratio_ref, 1)
    later = halo_copies(ratio_ref, 1)
    for copy in later:
        copy.start()
    for copy in later:
        copy.wait_recv()
    clear_borders(1)
    convolve(ratio_ref, 1, True)
    for group in (0, 1):
        at = pl.ds(4 * group, 4)
        updated = est_ref[at] * inverse(group)
        updated_ref[at] = updated
        for pair in (0, 1):
            pool_a[2 * group + pair] = updated[2 * pair] + updated[2 * pair + 1]

    even, odd = pl.ds(0, ROWS // 2, stride=2), pl.ds(1, ROWS // 2, stride=2)
    level_one = [(pool_a[k, even, :] + pool_a[k, odd, :]) * 0.25 for k in range(4)]
    for k in (0, 1):
        pool_b[k] = level_one[2 * k] + level_one[2 * k + 1]
    even, odd = pl.ds(0, ROWS // 4, stride=2), pl.ds(1, ROWS // 4, stride=2)
    level_two = [(pool_b[k, even, :] + pool_b[k, odd, :]) * 0.25 for k in (0, 1)]
    pool_c[...] = level_two[0] + level_two[1]
    even, odd = pl.ds(0, ROWS // 8, stride=2), pl.ds(1, ROWS // 8, stride=2)
    level_three = (pool_c[even, :] + pool_c[odd, :]) * 0.25
    pool_d[0:8] = level_three
    pool_d[8:16] = jnp.zeros((8, 128), F32)
    even, odd = pl.ds(0, 8, stride=2), pl.ds(1, 8, stride=2)
    level_four = (pool_d[even, :] + pool_d[odd, :]) * 0.5
    plane_ref[0] = dot(exact_triple(level_four), pools_ref[:, 384:])
    swap = pltpu.make_async_remote_copy(
        src_ref=plane_ref.at[0],
        dst_ref=plane_ref.at[1],
        send_sem=ring_send.at[0],
        recv_sem=ring_recv.at[0],
        device_id=device(0, 0, 1),
        device_id_type=MESH,
    )
    swap.start()
    third = dot(exact_triple(level_three), pools_ref[:, 256:384])
    three_ref[0] = third[:, :16]
    second = dot(exact_triple(jnp.concatenate(level_two, axis=0)), pools_ref[:, 128:256])
    for k in (0, 1):
        two_ref[k] = second[16 * k : 16 * k + 16, :32]
    full = dot(exact_triple(jnp.concatenate(level_one, axis=0)), pools_ref[:, :128])
    for k in range(4):
        one_ref[k] = full[32 * k : 32 * k + 32, :64]
    swap.wait_recv()
    fourth = (plane_ref[0] + plane_ref[1]) * 0.5
    four_ref[0] = fourth[:4, :8]
    pool_d[0:8] = fourth
    fifth = pool_d[even, :] + pool_d[odd, :]
    source = lax.broadcasted_iota(jnp.int32, (384, 128), 0) % 128
    target = lax.broadcasted_iota(jnp.int32, (384, 128), 1)
    place = (source < 8) & (target == 4 * gy + source // 2)
    tile_ref[0] = dot(exact_triple(fifth), jnp.where(place, 0.25, 0.0).astype(BF16))

    def tile_copy(k):
        return pltpu.make_async_remote_copy(
            src_ref=tile_ref.at[0],
            dst_ref=tile_ref.at[k],
            send_sem=ring_send.at[k],
            recv_sem=ring_recv.at[k],
            device_id=device(0, k),
            device_id_type=MESH,
        )

    def strip_copy(k):
        return pltpu.make_async_remote_copy(
            src_ref=strips_ref.at[gx],
            dst_ref=strips_ref.at[gx],
            send_sem=ring_send.at[ny + k],
            recv_sem=ring_recv.at[ny + k],
            device_id=device(k, 0),
            device_id_type=MESH,
        )

    def strip_wait(k):
        slot = strips_ref.at[lax.rem(gx - k + nx, nx)]
        pltpu.make_async_remote_copy(
            src_ref=slot,
            dst_ref=slot,
            send_sem=ring_send.at[ny + k],
            recv_sem=ring_recv.at[ny + k],
            device_id=device(k, 0),
            device_id_type=MESH,
        ).wait_recv()

    for k in range(1, ny):
        tile_copy(k).start()
    strip = tile_ref[0]
    for k in range(1, ny):
        tile_copy(k).wait_recv()
        strip = strip + tile_ref[k]
    strips_ref[gx] = strip
    for k in range(1, nx):
        strip_copy(k).start()
    for k in range(1, nx):
        strip_wait(k)
    for g in range(nx):
        five_ref[0, 2 * g : 2 * g + 2, :] = strips_ref[g, 0:2, : 4 * ny]

    for copy in copies + later:
        copy.wait_send()
    for turn in (0, 1):
        for z in range(8):
            partner_copy(turn, z).wait_send()
    swap.wait_send()
    for k in range(1, ny):
        tile_copy(k).wait_send()
    for k in range(1, nx):
        strip_copy(k).wait_send()


def local(nx, ny, estimate, view_data, psf_stack, view_index):
    vmem = pl.BlockSpec(memory_space=pltpu.VMEM)
    shape = jax.ShapeDtypeStruct
    constants = [jnp.asarray(t) for t in tables()]
    return pl.pallas_call(
        functools.partial(body, nx, ny),
        out_shape=(
            shape((8, 64, 128), F32),
            shape((4, 32, 64), F32),
            shape((2, 16, 32), F32),
            shape((1, 8, 16), F32),
            shape((1, 4, 8), F32),
            shape((1, 2 * nx, 4 * ny), F32),
        ),
        in_specs=[
            pl.BlockSpec(memory_space=pltpu.SMEM),
            vmem,
            vmem,
            pl.BlockSpec(memory_space=pl.ANY),
        ]
        + [vmem] * len(constants),
        out_specs=(vmem,) * 6,
        scratch_shapes=[
            pltpu.VMEM(psf_stack.shape, F32),
            pltpu.VMEM((32, 32, 128), F32),
            pltpu.VMEM((32, 32, 256), F32),
            pltpu.VMEM((32, 2 * LX, 128), F32),
            pltpu.VMEM((8, ROWS, COLUMNS), F32),
            pltpu.VMEM((2, 2, 8, EDGE, 128), F32),
            pltpu.VMEM((2, 2, LX, 128), F32),
            pltpu.VMEM((2, 2, ROWS, 128), F32),
            pltpu.VMEM((2, 8, 2 * LX, 128), F32),
            pltpu.VMEM((2, 8, 2 * LX, 128), F32),
            pltpu.VMEM((8, 2 * LX, 128), F32),
            pltpu.VMEM((4, 64, 128), F32),
            pltpu.VMEM((2, 32, 128), F32),
            pltpu.VMEM((16, 128), F32),
            pltpu.VMEM((16, 128), F32),
            pltpu.VMEM((2, 8, 128), F32),
            pltpu.VMEM((ny, 8, 128), F32),
            pltpu.VMEM((nx, 8, 128), F32),
            pltpu.SemaphoreType.DMA,
            pltpu.SemaphoreType.DMA((2, 8)),
            pltpu.SemaphoreType.DMA((2, 8)),
            pltpu.SemaphoreType.DMA((2, 8)),
            pltpu.SemaphoreType.DMA((2, 8)),
            pltpu.SemaphoreType.DMA((nx + ny,)),
            pltpu.SemaphoreType.DMA((nx + ny,)),
        ],
        compiler_params=pltpu.CompilerParams(collective_id=0, has_side_effects=True),
    )(view_index, estimate, view_data, psf_stack, *constants)


def solution(mesh):
    spread = P("gz", "gx", "gy")
    return jax.shard_map(
        functools.partial(local, mesh.shape["gx"], mesh.shape["gy"]),
        mesh=mesh,
        in_specs=(spread, spread, P(), P()),
        out_specs=(spread, spread, spread, spread, P(None, "gx", "gy"), P()),
        check_vma=False,
    )
```

profile of v0, /device:TPU:1, one launch (start us, length us, event | category | flops | bytes accessed | tf_op | source)
XLA Modules:
  0.0 53.6 jit_solution(6481127396643928080)
XLA Ops:
  1.3 44.0 %shard_map.163 = (f32[8,64,128]{2,1,0:T(8,128)}, f32[4,32,64]{2,1,0:T(8,128)}, f32[2,16,32]{2,1,0:T(8,128)}, f32[1,8,16]{2,1,0:T(8,128)}, f32[1,4,8]{2,1,0:T(4,128)}, /*index=5*/f32[1,32,32]{2,1,0:T(8,128)}) custom-call(s32[1]{0:T(128)S(6)} %copy.24.index_ref, f32[8,64,128]{2,1,0:T(8,128)} %est_ref.1, f32[8,64,128]{2,1,0:T(8,128)} %view_ref.1, ...), custom_call_target="tpu_custom_call" | custom-call | tf_op jit(solution)/shard_map/pallas_call | solution.py:509
  45.3 1.7 %copy.25 = f32[8,64,128]{2,1,0:T(8,128)} copy(f32[8,64,128]{2,1,0:T(8,128)} %get-tuple-element.12) | data formatting | bytes 524288
  47.0 1.5 %copy.26 = f32[4,32,64]{2,1,0:T(8,128)} copy(f32[4,32,64]{2,1,0:T(8,128)} %get-tuple-element.13) | data formatting | bytes 65536
  48.4 1.3 %copy.27 = f32[2,16,32]{2,1,0:T(8,128)} copy(f32[2,16,32]{2,1,0:T(8,128)} %get-tuple-element.14) | data formatting | bytes 8192
  49.8 1.3 %copy.28 = f32[1,8,16]{2,1,0:T(8,128)} copy(f32[1,8,16]{2,1,0:T(8,128)} %get-tuple-element.15) | data formatting | bytes 1024
  51.0 1.2 %copy.29 = f32[1,4,8]{2,1,0:T(4,128)} copy(f32[1,4,8]{2,1,0:T(4,128)} %get-tuple-element.16) | data formatting | bytes 256
  52.3 1.3 %copy.30 = f32[1,32,32]{2,1,0:T(8,128)} copy(f32[1,32,32]{2,1,0:T(8,128)} %get-tuple-element.17) | data formatting | bytes 8192
where the time goes:
time: 54 us; the launch traced here: 53.6 us
  Pallas kernels  44 us (81%)
  local copies, waits for them, and re-layouts  8.3 us (15%)
  between operations  1.29 us (2%)
    pallas_call x1, Pallas kernels, local(): pl.pallas_call(functools.partial(body, nx, ny), out_shape=(shape((8, 64,...  44 us
    unnamed x6, local copies, waits for them, and re-layouts  8.3 us

commit v1 on v0

--- a/solution.py
+++ b/solution.py
@@ -108,53 +108,53 @@
     return jnp.concatenate([high, middle, low], axis=1)
 
 
-def body(
-    nx,
-    ny,
-    index_ref,
-    est_ref,
-    view_ref,
-    psf_hbm,
-    first_ref,
-    second_ref,
-    rows_ref,
-    rows_back_ref,
-    columns_back_ref,
-    tap_columns_ref,
-    tap_rows_ref,
-    pools_ref,
-    updated_ref,
-    one_ref,
-    two_ref,
-    three_ref,
-    four_ref,
-    five_ref,
-    psf_ref,
-    taps_ref,
-    tap_half_ref,
-    kernel_ref,
-    ratio_ref,
-    edge_rows,
-    edge_columns,
-    packed,
-    own_ref,
-    other_ref,
-    product_ref,
-    pool_a,
-    pool_b,
-    pool_c,
-    pool_d,
-    plane_ref,
-    tile_ref,
-    strips_ref,
-    local_sem,
-    send_sem,
-    recv_sem,
-    part_send,
-    part_recv,
-    ring_send,
-    ring_recv,
-):
+def body(nx, ny, index_ref, *refs):
+    inputs, refs = refs[:11], refs[11:]
+    updated_ref, one_ref, two_ref, three_ref, four_ref, five_ref = refs[:6]
+    held, refs = refs[6:17], refs[17:]
+    (
+        est_ref,
+        view_ref,
+        psf_ref,
+        first_ref,
+        second_ref,
+        rows_ref,
+        rows_back_ref,
+        columns_back_ref,
+        tap_columns_ref,
+        tap_rows_ref,
+        pools_ref,
+    ) = held
+    (
+        taps_ref,
+        tap_half_ref,
+        kernel_ref,
+        ratio_ref,
+        edge_rows,
+        edge_columns,
+        packed,
+        own_ref,
+        other_ref,
+        product_ref,
+        pool_a,
+        pool_b,
+        pool_c,
+        pool_d,
+        plane_ref,
+        tile_ref,
+        gathered,
+        local_sem,
+        send_sem,
+        recv_sem,
+        part_send,
+        part_recv,
+        swap_send,
+        swap_recv,
+        all_send,
+        all_recv,
+        wider_sem,
+        widest_sem,
+    ) = refs
     gx, gy, gz = lax.axis_index("gx"), lax.axis_index("gy"), lax.axis_index("gz")
 
     def device(dx, dy, dz=0):
@@ -164,16 +164,36 @@
             "gz": lax.rem(gz + dz, 2),
         }
 
-    fetch = pltpu.make_async_copy(psf_hbm, psf_ref, local_sem)
-    fetch.start()
+    fetches = [
+        pltpu.make_async_copy(source, target, local_sem.at[k])
+        for k, (source, target) in enumerate(zip(inputs, held))
+    ]
+    fetches[0].start()
 
     peers = [(dx, dy, 0) for dx in (-1, 0, 1) for dy in (-1, 0, 1) if (dx, dy) != (0, 0)]
     peers.append((0, 0, 1))
-    peers += [(0, k, 0) for k in range(2, ny - 1)]
-    peers += [(k, 0, 0) for k in range(2, nx - 1)]
+    count = nx * ny
+    centre = (nx // 2) * ny + ny // 2
     barrier = pltpu.get_barrier_semaphore()
     for peer in peers:
         pl.semaphore_signal(barrier, inc=1, device_id=device(*peer), device_id_type=MESH)
+    for k in (2, 8, 9, 3, 4, 5, 6, 7, 1, 10):
+        fetches[k].start()
+
+    def far(k):
+        dx, dy = k // ny + nx // 2, lax.rem(k, ny) + ny // 2
+        return lax.rem(dx, nx), lax.rem(dy, ny)
+
+    def over_far(step):
+        lax.fori_loop(0, centre, step, 0)
+        lax.fori_loop(centre + 1, count, step, 0)
+
+    def spread_word(sem, offsets):
+        for dx, dy in offsets:
+            pl.semaphore_signal(sem, inc=1, device_id=device(dx, dy), device_id_type=MESH)
+
+    wider = [(dx, dy) for dx in (-2, 0, 2) for dy in (-2, 0, 2) if (dx, dy) != (0, 0)]
+    widest = [(-4, 0), (4, 0)]
 
     def pack(source, turn):
         lane = lax.broadcasted_iota(jnp.int32, (ROWS, 128), 1)
@@ -334,7 +354,8 @@
         depth(other_ref, turn, base, mirrored, True)
 
     def spectrum():
-        fetch.wait()
+        for k in (2, 8, 9):
+            fetches[k].wait()
         view = index_ref[0]
         taps_ref[...] = jnp.zeros((32, 32, 128), F32)
 
@@ -375,6 +396,7 @@
 
         lax.fori_loop(0, 16, rows, 0)
 
+    fetches[0].wait()
     pack(est_ref, 0)
     pl.semaphore_wait(barrier, len(peers))
     copies = halo_copies(est_ref, 0)
@@ -383,12 +405,17 @@
     spectrum()
     for copy in copies:
         copy.wait_recv()
+    spread_word(wider_sem, wider)
     clear_borders(0)
+    for k in (3, 4, 5, 6, 7, 1, 10):
+        fetches[k].wait()
     convolve(est_ref, 0, False)
     for group in (0, 1):
         at = pl.ds(4 * group, 4)
         ratio_ref[at] = view_ref[at] / inverse(group)
 
+    pl.semaphore_wait(wider_sem, len(wider))
+    spread_word(widest_sem, widest)
     pack(ratio_ref, 1)
     later = halo_copies(ratio_ref, 1)
     for copy in later:
@@ -421,8 +448,8 @@
     swap = pltpu.make_async_remote_copy(
         src_ref=plane_ref.at[0],
         dst_ref=plane_ref.at[1],
-        send_sem=ring_send.at[0],
-        recv_sem=ring_recv.at[0],
+        send_sem=swap_send,
+        recv_sem=swap_recv,
         device_id=device(0, 0, 1),
         device_id_type=MESH,
     )
@@ -443,52 +470,37 @@
     source = lax.broadcasted_iota(jnp.int32, (384, 128), 0) % 128
     target = lax.broadcasted_iota(jnp.int32, (384, 128), 1)
     place = (source < 8) & (target == 4 * gy + source // 2)
-    tile_ref[0] = dot(exact_triple(fifth), jnp.where(place, 0.25, 0.0).astype(BF16))
-
-    def tile_copy(k):
-        return pltpu.make_async_remote_copy(
-            src_ref=tile_ref.at[0],
-            dst_ref=tile_ref.at[k],
-            send_sem=ring_send.at[k],
-            recv_sem=ring_recv.at[k],
-            device_id=device(0, k),
+    placed = dot(exact_triple(fifth), jnp.where(place, 0.25, 0.0).astype(BF16))
+    tile_ref[...] = placed[0:1] + pltpu.roll(placed[1:2], 4 * ny, 1)
+    me = gx * ny + gy
+
+    def send(k, carry):
+        pltpu.make_async_remote_copy(
+            src_ref=tile_ref,
+            dst_ref=gathered.at[me],
+            send_sem=all_send,
+            recv_sem=all_recv,
+            device_id=device(*far(k)),
             device_id_type=MESH,
-        )
-
-    def strip_copy(k):
-        return pltpu.make_async_remote_copy(
-            src_ref=strips_ref.at[gx],
-            dst_ref=strips_ref.at[gx],
-            send_sem=ring_send.at[ny + k],
-            recv_sem=ring_recv.at[ny + k],
-            device_id=device(k, 0),
-            device_id_type=MESH,
-        )
-
-    def strip_wait(k):
-        slot = strips_ref.at[lax.rem(gx - k + nx, nx)]
-        pltpu.make_async_remote_copy(
-            src_ref=slot,
-            dst_ref=slot,
-            send_sem=ring_send.at[ny + k],
-            recv_sem=ring_recv.at[ny + k],
-            device_id=device(k, 0),
-            device_id_type=MESH,
-        ).wait_recv()
-
-    for k in range(1, ny):
-        tile_copy(k).start()
-    strip = tile_ref[0]
-    for k in range(1, ny):
-        tile_copy(k).wait_recv()
-        strip = strip + tile_ref[k]
-    strips_ref[gx] = strip
-    for k in range(1, nx):
-        strip_copy(k).start()
-    for k in range(1, nx):
-        strip_wait(k)
-    for g in range(nx):
-        five_ref[0, 2 * g : 2 * g + 2, :] = strips_ref[g, 0:2, : 4 * ny]
+        ).start()
+        return carry
+
+    pl.semaphore_wait(widest_sem, len(widest))
+    over_far(send)
+    gathered[me] = tile_ref[...]
+    others = gathered.at[pl.ds(0, count - 1)]
+    everyone = pltpu.make_async_remote_copy(
+        src_ref=others,
+        dst_ref=others,
+        send_sem=all_send,
+        recv_sem=all_recv,
+        device_id=device(0, 1),
+        device_id_type=MESH,
+    )
+    everyone.wait_recv()
+    strips = jnp.sum(gathered[...].reshape(nx, ny, 128), axis=1)
+    five_ref[0, pl.ds(0, nx, stride=2), :] = strips[:, : 4 * ny]
+    five_ref[0, pl.ds(1, nx, stride=2), :] = pltpu.roll(strips, 128 - 4 * ny, 1)[:, : 4 * ny]
 
     for copy in copies + later:
         copy.wait_send()
@@ -496,36 +508,48 @@
         for z in range(8):
             partner_copy(turn, z).wait_send()
     swap.wait_send()
-    for k in range(1, ny):
-        tile_copy(k).wait_send()
-    for k in range(1, nx):
-        strip_copy(k).wait_send()
+    everyone.wait_send()
+
+
+def hand_over(*refs):
+    sources, targets, sems = refs[:6], refs[6:12], refs[12]
+    copies = [pltpu.make_async_copy(a, b, sems.at[k]) for k, (a, b) in enumerate(zip(sources, targets))]
+    for copy in copies:
+        copy.start()
+    for copy in copies:
+        copy.wait()
 
 
 def local(nx, ny, estimate, view_data, psf_stack, view_index):
     vmem = pl.BlockSpec(memory_space=pltpu.VMEM)
+    anywhere = pl.BlockSpec(memory_space=pl.ANY)
     shape = jax.ShapeDtypeStruct
+    out_shape = (
+        shape((8, 64, 128), F32),
+        shape((4, 32, 64), F32),
+        shape((2, 16, 32), F32),
+        shape((1, 8, 16), F32),
+        shape((1, 4, 8), F32),
+        shape((1, 2 * nx, 4 * ny), F32),
+    )
     constants = [jnp.asarray(t) for t in tables()]
-    return pl.pallas_call(
+    kept = [
+        pltpu.with_memory_space_constraint(x, pltpu.HBM)
+        for x in (estimate, view_data, psf_stack, *constants)
+    ]
+    results = pl.pallas_call(
         functools.partial(body, nx, ny),
-        out_shape=(
-            shape((8, 64, 128), F32),
-            shape((4, 32, 64), F32),
-            shape((2, 16, 32), F32),
-            shape((1, 8, 16), F32),
-            shape((1, 4, 8), F32),
-            shape((1, 2 * nx, 4 * ny), F32),
-        ),
-        in_specs=[
-            pl.BlockSpec(memory_space=pltpu.SMEM),
-            vmem,
-            vmem,
-            pl.BlockSpec(memory_space=pl.ANY),
-        ]
-        + [vmem] * len(constants),
+        out_shape=out_shape,
+        in_specs=[pl.BlockSpec(memory_space=pltpu.SMEM)]
+        + [pl.BlockSpec(memory_space=pltpu.HBM)] * len(kept),
         out_specs=(vmem,) * 6,
         scratch_shapes=[
+            pltpu.VMEM(estimate.shape, F32),
+            pltpu.VMEM(view_data.shape, F32),
             pltpu.VMEM(psf_stack.shape, F32),
+        ]
+        + [pltpu.VMEM(c.shape, c.dtype) for c in constants]
+        + [
             pltpu.VMEM((32, 32, 128), F32),
             pltpu.VMEM((32, 32, 256), F32),
             pltpu.VMEM((32, 2 * LX, 128), F32),
@@ -541,18 +565,32 @@
             pltpu.VMEM((16, 128), F32),
             pltpu.VMEM((16, 128), F32),
             pltpu.VMEM((2, 8, 128), F32),
-            pltpu.VMEM((ny, 8, 128), F32),
-            pltpu.VMEM((nx, 8, 128), F32),
-            pltpu.SemaphoreType.DMA,
+            pltpu.VMEM((1, 128), F32),
+            pltpu.VMEM((nx * ny, 1, 128), F32),
+            pltpu.SemaphoreType.DMA((len(kept),)),
             pltpu.SemaphoreType.DMA((2, 8)),
             pltpu.SemaphoreType.DMA((2, 8)),
             pltpu.SemaphoreType.DMA((2, 8)),
             pltpu.SemaphoreType.DMA((2, 8)),
-            pltpu.SemaphoreType.DMA((nx + ny,)),
-            pltpu.SemaphoreType.DMA((nx + ny,)),
+            pltpu.SemaphoreType.DMA,
+            pltpu.SemaphoreType.DMA,
+            pltpu.SemaphoreType.DMA,
+            pltpu.SemaphoreType.DMA,
+            pltpu.SemaphoreType.REGULAR,
+            pltpu.SemaphoreType.REGULAR,
         ],
-        compiler_params=pltpu.CompilerParams(collective_id=0, has_side_effects=True),
-    )(view_index, estimate, view_data, psf_stack, *constants)
+        compiler_params=pltpu.CompilerParams(
+            collective_id=0, has_side_effects=True, vmem_limit_bytes=32 << 20
+        ),
+    )(view_index, *kept)
+    return pl.pallas_call(
+        hand_over,
+        out_shape=out_shape,
+        in_specs=[vmem] * 6,
+        out_specs=(anywhere,) * 6,
+        scratch_shapes=[pltpu.SemaphoreType.DMA((6,))],
+        compiler_params=pltpu.CompilerParams(vmem_limit_bytes=4 << 20),
+    )(*results)
 
 
 def solution(mesh):

time: 54 us -> 43.4 us (0.80)
  local copies, waits for them, and re-layouts: 8.3 us -> 0 us
  Pallas kernels: 44 us -> 42 us
    unnamed x6 -> x0, local copies, waits for them, and re-layouts: 8.3 us -> none
    pallas_call x1 -> x2, Pallas kernels: 44 us -> 42 us  [the longest x1 41.3 us: local(): pl.pallas_call(functools.partial(body, nx, ny), out_shape=out_shape, in_s...]
where the time goes in v1:
time: 43.4 us; the launch traced here: 43.3 us
  Pallas kernels  42 us (97%)
  between operations  1.29 us (3%)
    pallas_call x1, Pallas kernels, local(): pl.pallas_call(functools.partial(body, nx, ny), out_shape=out_shape, in_s...  41.3 us

profile of v1, /device:TPU:1, one launch (start us, length us, event | category | flops | bytes accessed | tf_op | source)
XLA Modules:
  0.0 43.3 jit_solution(3118180141696608972)
XLA Ops:
  1.3 41.3 %shard_map.163 = (f32[8,64,128]{2,1,0:T(8,128)S(1)}, f32[4,32,64]{2,1,0:T(8,128)S(1)}, f32[2,16,32]{2,1,0:T(8,128)S(1)}, f32[1,8,16]{2,1,0:T(8,128)S(1)}, f32[1,...) custom-call(s32[1]{0:T(128)S(6)} %copy.18.index_ref, f32[8,64,128]{2,1,0:T(8,128)} %refs_0_.1, f32[8,64,128]{2,1,0:T(8,128)} %refs_1_.1, ...), custom_call_target="tpu_custom_call" | custom-call | tf_op jit(solution)/shard_map/pallas_call | solution.py:540
  42.5 0.8 %shard_map.164 = (f32[8,64,128]{2,1,0:T(8,128)}, f32[4,32,64]{2,1,0:T(8,128)}, f32[2,16,32]{2,1,0:T(8,128)}, f32[1,8,16]{2,1,0:T(8,128)}, f32[1,4,8]{2,1,0:T(4,128)}, /*index=5*/f32[1,32,32]{2,1,0:T(8,128)}) custom-call(f32[8,64,128]{2,1,0:T(8,128)S(1)} %get-tuple-element.12.refs_0_, f32[4,32,64]{2,1,0:T(8,128)S(1)} %get-tuple-element.13.refs_1_, ...), custom_call_target="tpu_custom_call" | custom-call | tf_op jit(solution)/shard_map/pallas_call | solution.py:586

commit v2 on v1

--- a/solution.py
+++ b/solution.py
@@ -55,7 +55,8 @@
     right = column_table(LY - EDGE + np.arange(EDGE))
     first = stacked(np.concatenate([inner] + [left, right] * 4))
     second = stacked(np.concatenate([inner] + [right, left] * 4))
-    rows = beside(row_table(np.arange(LX)))
+    inner_rows = beside(row_table(EDGE + np.arange(ROWS)))
+    edge_rows = beside(row_table(np.concatenate([np.arange(EDGE), LX - EDGE + np.arange(EDGE)])))
     angle = 2.0 * np.pi / LX * np.outer(EDGE + np.arange(ROWS), np.arange(LX))
     c, s = np.cos(angle), np.sin(angle)
     rows_back = beside(np.block([[c, -s], [s, c]]))
@@ -64,7 +65,8 @@
     back = np.zeros((256, COLUMNS))
     back[:HALF] = weight * np.cos(angle)
     back[128 : 128 + HALF] = -weight * np.sin(angle)
-    columns_back = stacked(back)
+    high, low = parts_of(back)
+    columns_back = np.block([[high, low], [high, np.zeros_like(low)]])
     taps = column_table(np.concatenate([np.arange(TAPS) - HALO, [0]]))
     taps[TAPS] = 0.0
     tap_columns = np.concatenate([stacked(taps), np.zeros((32, 256), BF16)], axis=0)
@@ -78,7 +80,17 @@
         for column in range(COLUMNS):
             pools[column, 128 * level + column // step] = 1.0 / step
     pools = np.concatenate([pools] * 3, axis=0).astype(BF16)
-    return first, second, rows, rows_back, columns_back, tap_columns, tap_rows, pools
+    return (
+        first,
+        second,
+        inner_rows,
+        edge_rows,
+        rows_back,
+        columns_back,
+        tap_columns,
+        tap_rows,
+        pools,
+    )
 
 
 def two(x):
@@ -109,16 +121,17 @@
 
 
 def body(nx, ny, index_ref, *refs):
-    inputs, refs = refs[:11], refs[11:]
+    inputs, refs = refs[:12], refs[12:]
     updated_ref, one_ref, two_ref, three_ref, four_ref, five_ref = refs[:6]
-    held, refs = refs[6:17], refs[17:]
+    held, refs = refs[6:18], refs[18:]
     (
         est_ref,
         view_ref,
         psf_ref,
         first_ref,
         second_ref,
-        rows_ref,
+        inner_rows_ref,
+        edge_rows_ref,
         rows_back_ref,
         columns_back_ref,
         tap_columns_ref,
@@ -157,12 +170,14 @@
     ) = refs
     gx, gy, gz = lax.axis_index("gx"), lax.axis_index("gy"), lax.axis_index("gz")
 
+    def turned(at, offset, length):
+        offset = offset % length
+        if offset == 0:
+            return at
+        return jnp.where(at >= length - offset, at + offset - length, at + offset)
+
     def device(dx, dy, dz=0):
-        return {
-            "gx": lax.rem(gx + dx + nx, nx),
-            "gy": lax.rem(gy + dy + ny, ny),
-            "gz": lax.rem(gz + dz, 2),
-        }
+        return {"gx": turned(gx, dx, nx), "gy": turned(gy, dy, ny), "gz": turned(gz, dz, 2)}
 
     fetches = [
         pltpu.make_async_copy(source, target, local_sem.at[k])
@@ -173,20 +188,18 @@
     peers = [(dx, dy, 0) for dx in (-1, 0, 1) for dy in (-1, 0, 1) if (dx, dy) != (0, 0)]
     peers.append((0, 0, 1))
     count = nx * ny
-    centre = (nx // 2) * ny + ny // 2
+
+    def hops(offset):
+        dx, dy = offset
+        ring = lambda k, n: min(k, n - k)
+        return ring(dx % 4, 4) + ring(dx // 4, nx // 4) + ring(dy, ny)
+
+    far = sorted(((dx, dy) for dx in range(nx) for dy in range(ny)), key=hops, reverse=True)[:-1]
     barrier = pltpu.get_barrier_semaphore()
     for peer in peers:
         pl.semaphore_signal(barrier, inc=1, device_id=device(*peer), device_id_type=MESH)
-    for k in (2, 8, 9, 3, 4, 5, 6, 7, 1, 10):
+    for k in (2, 9, 10, 3, 4, 5, 6, 7, 8, 1, 11):
         fetches[k].start()
-
-    def far(k):
-        dx, dy = k // ny + nx // 2, lax.rem(k, ny) + ny // 2
-        return lax.rem(dx, nx), lax.rem(dy, ny)
-
-    def over_far(step):
-        lax.fori_loop(0, centre, step, 0)
-        lax.fori_loop(centre + 1, count, step, 0)
 
     def spread_word(sem, offsets):
         for dx, dy in offsets:
@@ -195,14 +208,17 @@
     wider = [(dx, dy) for dx in (-2, 0, 2) for dy in (-2, 0, 2) if (dx, dy) != (0, 0)]
     widest = [(-4, 0), (4, 0)]
 
-    def pack(source, turn):
+    def pack(source, turn, group):
         lane = lax.broadcasted_iota(jnp.int32, (ROWS, 128), 1)
-        to_right = jnp.zeros((ROWS, 128), F32)
-        to_left = jnp.zeros((ROWS, 128), F32)
-        for z in range(8):
-            base = (z % 4) * 32
-            low, high = (base, base + EDGE) if z < 4 else (base + EDGE, base)
-            plane = source[z]
+        if group == 0:
+            to_right = jnp.zeros((ROWS, 128), F32)
+            to_left = jnp.zeros((ROWS, 128), F32)
+        else:
+            to_right, to_left = packed[turn, 0], packed[turn, 1]
+        for j in range(4):
+            base = 32 * j
+            low, high = (base, base + EDGE) if group == 0 else (base + EDGE, base)
+            plane = source[4 * group + j]
             shift = (low - (COLUMNS - EDGE)) % 128
             rolled = pltpu.roll(plane, shift, 1) if shift else plane
             to_right = jnp.where((lane >= low) & (lane < low + EDGE), rolled, to_right)
@@ -227,18 +243,36 @@
 
         right, left = packed.at[turn, 0], packed.at[turn, 1]
         from_left, from_right = edge_columns.at[turn, 0], edge_columns.at[turn, 1]
-        return [
-            copy(source.at[:, tail, :], edge_rows.at[turn, 0], 0, 1, 0),
-            copy(source.at[:, head, :], edge_rows.at[turn, 1], 1, -1, 0),
-            copy(right.at[tail, :], from_left.at[top, :], 2, 1, 1),
-            copy(right.at[head, :], from_left.at[bottom, :], 3, -1, 1),
-            copy(left.at[tail, :], from_right.at[top, :], 4, 1, -1),
-            copy(left.at[head, :], from_right.at[bottom, :], 5, -1, -1),
-            copy(right, from_left.at[middle, :], 6, 0, 1),
-            copy(left, from_right.at[middle, :], 7, 0, -1),
+        along = []
+        for group in (0, 1):
+            planes = pl.ds(4 * group, 4)
+            into = edge_rows.at[turn, 0, planes], edge_rows.at[turn, 1, planes]
+            along.append(copy(source.at[planes, tail, :], into[0], 2 * group, 1, 0))
+            along.append(copy(source.at[planes, head, :], into[1], 2 * group + 1, -1, 0))
+        corners = [
+            copy(right.at[tail, :], from_left.at[top, :], 4, 1, 1),
+            copy(right.at[head, :], from_left.at[bottom, :], 5, -1, 1),
+            copy(left.at[tail, :], from_right.at[top, :], 6, 1, -1),
+            copy(left.at[head, :], from_right.at[bottom, :], 7, -1, -1),
         ]
-
-    def clear_borders(turn):
+        across = [
+            copy(right, from_left.at[middle, :], 8, 0, 1),
+            copy(left, from_right.at[middle, :], 9, 0, -1),
+        ]
+        return along, corners, across
+
+    def clear_columns(turn, rows, height):
+        @pl.when(gy == 0)
+        def _():
+            for at in rows:
+                edge_columns[turn, 0, at, :] = jnp.zeros((height, 128), F32)
+
+        @pl.when(gy == ny - 1)
+        def _():
+            for at in rows:
+                edge_columns[turn, 1, at, :] = jnp.zeros((height, 128), F32)
+
+    def clear_rows(turn):
         @pl.when(gx == 0)
         def _():
             edge_rows[turn, 0] = jnp.zeros((8, EDGE, 128), F32)
@@ -251,13 +285,7 @@
             for side in (0, 1):
                 edge_columns[turn, side, bottom, :] = jnp.zeros((EDGE, 128), F32)
 
-        @pl.when(gy == 0)
-        def _():
-            edge_columns[turn, 0] = jnp.zeros((LX, 128), F32)
-
-        @pl.when(gy == ny - 1)
-        def _():
-            edge_columns[turn, 1] = jnp.zeros((LX, 128), F32)
+        clear_columns(turn, (top, bottom), EDGE)
 
     def partner_copy(turn, z):
         return pltpu.make_async_remote_copy(
@@ -269,24 +297,19 @@
             device_id_type=MESH,
         )
 
-    def forward(source, turn):
-        lane = lax.broadcasted_iota(jnp.int32, (LX, 128), 1)
+    def transform(turn, height, plane_of, left, right, rows_table, adding):
+        lane = lax.broadcasted_iota(jnp.int32, (height, 128), 1)
         even = (lane & EDGE) == 0
-        left, right = edge_columns[turn, 0], edge_columns[turn, 1]
         for group, table in ((0, first_ref), (1, second_ref)):
             mixed = jnp.where(even, left, right) if group == 0 else jnp.where(even, right, left)
             rows = []
             for j in range(4):
-                z = 4 * group + j
-                plane = jnp.concatenate(
-                    [edge_rows[turn, 0, z], source[z], edge_rows[turn, 1, z]], axis=0
-                )
                 side = jnp.where((lane >= 32 * j) & (lane < 32 * j + 32), mixed, 0.0)
-                rows.append(jnp.concatenate([plane, side], axis=1))
+                rows.append(jnp.concatenate([plane_of(4 * group + j), side], axis=1))
             half = dot(left_triple(jnp.concatenate(rows, axis=0)), table[...])
             for pair in (0, 1):
-                a = half[192 * pair : 192 * pair + 96]
-                b = half[192 * pair + 96 : 192 * pair + 192]
+                a = half[2 * pair * height : (2 * pair + 1) * height]
+                b = half[(2 * pair + 1) * height : (2 * pair + 2) * height]
                 joint = jnp.concatenate(
                     [
                         jnp.concatenate([a[:, :128], b[:, :128]], axis=1),
@@ -294,12 +317,33 @@
                     ],
                     axis=0,
                 )
-                full = dot(rows_ref[...], right_triple(joint))
+                full = dot(rows_table[...], right_triple(joint))
                 z = 4 * group + 2 * pair
-                own_ref[turn, z] = full[:, :128]
-                own_ref[turn, z + 1] = full[:, 128:]
-                partner_copy(turn, z).start()
-                partner_copy(turn, z + 1).start()
+                for b in (0, 1):
+                    part = full[:, 128 * b : 128 * b + 128]
+                    if adding:
+                        own_ref[turn, z + b] = own_ref[turn, z + b] + part
+                        partner_copy(turn, z + b).start()
+                    else:
+                        own_ref[turn, z + b] = part
+
+    def forward_inner(source, turn):
+        left, right = edge_columns[turn, 0, middle, :], edge_columns[turn, 1, middle, :]
+        transform(turn, ROWS, lambda z: source[z], left, right, inner_rows_ref, False)
+
+    def forward_edge(turn):
+        def both(a, b):
+            return jnp.concatenate([a, b], axis=0)
+
+        left, right = [
+            both(edge_columns[turn, side, top, :], edge_columns[turn, side, bottom, :])
+            for side in (0, 1)
+        ]
+
+        def plane_of(z):
+            return both(edge_rows[turn, 0, z], edge_rows[turn, 1, z])
+
+        transform(turn, 2 * EDGE, plane_of, left, right, edge_rows_ref, True)
 
     def depth(x_ref, turn, base, mirrored, adding):
         def block(step, carry):
@@ -312,20 +356,24 @@
                 yi = [product_ref[z, im, :] for z in range(8)]
             else:
                 yr, yi = [None] * 8, [None] * 8
+            xs = [r + i for r, i in zip(xr, xi)]
+            sums = [[None] * 8 for _ in range(3)]
             for d in range(-7, 8):
-                kr, ki = kernel_ref[base + d, re, :], kernel_ref[base + d, im, :]
+                taps = [kernel_ref[base + d, pl.ds(at + LX * k, 8), :] for k in range(3)]
+                values = (xs, xi, xr) if mirrored else (xs, xr, xi)
                 for out in range(8):
                     z = out + d if mirrored else out - d
                     if not 0 <= z < 8:
                         continue
-                    if mirrored:
-                        r = kr * xr[z] + ki * xi[z]
-                        i = kr * xi[z] - ki * xr[z]
-                    else:
-                        r = kr * xr[z] - ki * xi[z]
-                        i = kr * xi[z] + ki * xr[z]
-                    yr[out] = r if yr[out] is None else yr[out] + r
-                    yi[out] = i if yi[out] is None else yi[out] + i
+                    for k in range(3):
+                        term = taps[k] * values[k][z]
+                        sums[k][out] = term if sums[k][out] is None else sums[k][out] + term
+            for z in range(8):
+                one, two_, three = (sums[k][z] for k in range(3))
+                r = one + two_ if mirrored else one - three
+                i = one - three if mirrored else one + two_
+                yr[z] = r if yr[z] is None else yr[z] + r
+                yi[z] = i if yi[z] is None else yi[z] + i
             for z in range(8):
                 product_ref[z, re, :] = yr[z]
                 product_ref[z, im, :] = yi[z]
@@ -342,11 +390,10 @@
             for b in (0, 1):
                 lanes = slice(128 * b, 128 * b + 128)
                 rows.append(jnp.concatenate([half[:ROWS, lanes], half[ROWS:, lanes]], axis=1))
-        full = dot(left_triple(jnp.concatenate(rows, axis=0)), columns_back_ref[...])
-        return full.reshape(4, ROWS, COLUMNS)
-
-    def convolve(source, turn, mirrored):
-        forward(source, turn)
+        full = dot(jnp.concatenate(two(jnp.concatenate(rows, axis=0)), axis=1), columns_back_ref[...])
+        return (full[:, :COLUMNS] + full[:, COLUMNS:]).reshape(4, ROWS, COLUMNS)
+
+    def convolve(turn, mirrored):
         depth(own_ref, turn, HALO, mirrored, False)
         for z in range(8):
             partner_copy(turn, z).wait_recv()
@@ -354,76 +401,88 @@
         depth(other_ref, turn, base, mirrored, True)
 
     def spectrum():
-        for k in (2, 8, 9):
+        for k in (2, 9, 10):
             fetches[k].wait()
         view = index_ref[0]
         taps_ref[...] = jnp.zeros((32, 32, 128), F32)
 
-        def load(z, total):
-            values = psf_ref[view, z]
-            taps_ref[z, 0:TAPS, 0:TAPS] = values
-            return total
-
-        lax.fori_loop(0, TAPS, load, 0)
+        taps_ref[0:TAPS, 0:TAPS, 0:TAPS] = psf_ref[view]
         total = jnp.sum(jnp.sum(taps_ref[...], axis=0), axis=(0, 1), keepdims=True)
         scale = 1.0 / total
 
-        def columns(step, carry):
-            x = taps_ref[pl.ds(step * 8, 8)].reshape(256, 128) * scale
+        for step in range(4):
+            x = taps_ref[8 * step : 8 * step + 8].reshape(256, 128) * scale
             high = x.astype(BF16).astype(F32)
             low = x - high
             joint = high + pltpu.roll(high, 32, 1) + pltpu.roll(low, 64, 1)
-            tap_half_ref[pl.ds(step * 8, 8)] = dot(joint.astype(BF16), tap_columns_ref[...]).reshape(
-                8, 32, 256
-            )
+            half = dot(joint.astype(BF16), tap_columns_ref[...])
+            tap_half_ref[8 * step : 8 * step + 8] = half.reshape(8, 32, 256)
+
+        def rows(step, carry):
+            for pair in range(4):
+                z = 8 * step + 2 * pair
+                a, b = tap_half_ref[z], tap_half_ref[z + 1]
+                joint = jnp.concatenate(
+                    [
+                        jnp.concatenate([a[:, :128], b[:, :128]], axis=1),
+                        jnp.concatenate([a[:, 128:], b[:, 128:]], axis=1),
+                    ],
+                    axis=0,
+                )
+                full = dot(tap_rows_ref[...], right_triple(joint))
+                for b in (0, 1):
+                    re = full[:LX, 128 * b : 128 * b + 128]
+                    im = full[LX:, 128 * b : 128 * b + 128]
+                    kernel_ref[z + b, 0:LX] = re
+                    kernel_ref[z + b, LX : 2 * LX] = im - re
+                    kernel_ref[z + b, 2 * LX :] = im + re
             return carry
 
-        lax.fori_loop(0, 4, columns, 0)
-
-        def rows(step, carry):
-            a, b = tap_half_ref[2 * step], tap_half_ref[2 * step + 1]
-            joint = jnp.concatenate(
-                [
-                    jnp.concatenate([a[:, :128], b[:, :128]], axis=1),
-                    jnp.concatenate([a[:, 128:], b[:, 128:]], axis=1),
-                ],
-                axis=0,
-            )
-            full = dot(tap_rows_ref[...], right_triple(joint))
-            kernel_ref[2 * step] = full[:, :128]
-            kernel_ref[2 * step + 1] = full[:, 128:]
-            return carry
-
-        lax.fori_loop(0, 16, rows, 0)
+        lax.fori_loop(0, 4, rows, 0)
 
     fetches[0].wait()
-    pack(est_ref, 0)
+    pack(est_ref, 0, 0)
+    pack(est_ref, 0, 1)
     pl.semaphore_wait(barrier, len(peers))
-    copies = halo_copies(est_ref, 0)
-    for copy in copies:
+    along, corners, across = halo_copies(est_ref, 0)
+    for copy in along + corners + across:
         copy.start()
     spectrum()
-    for copy in copies:
-        copy.wait_recv()
+    for k in (3, 4, 5, 6, 7, 8, 1, 11):
+        fetches[k].wait()
+
+    def receive(copies):
+        for copy in copies:
+            copy.wait_recv()
+
+    receive(across)
+    clear_columns(0, (middle,), ROWS)
+    forward_inner(est_ref, 0)
+    receive(along)
+    receive(corners)
     spread_word(wider_sem, wider)
-    clear_borders(0)
-    for k in (3, 4, 5, 6, 7, 1, 10):
-        fetches[k].wait()
-    convolve(est_ref, 0, False)
+    clear_rows(0)
+    forward_edge(0)
+    convolve(0, False)
+    late_along, late_corners, late_across = halo_copies(ratio_ref, 1)
     for group in (0, 1):
         at = pl.ds(4 * group, 4)
         ratio_ref[at] = view_ref[at] / inverse(group)
-
+        for copy in late_along[2 * group : 2 * group + 2]:
+            copy.start()
+        pack(ratio_ref, 1, group)
+    for copy in late_corners + late_across:
+        copy.start()
     pl.semaphore_wait(wider_sem, len(wider))
     spread_word(widest_sem, widest)
-    pack(ratio_ref, 1)
-    later = halo_copies(ratio_ref, 1)
-    for copy in later:
-        copy.start()
-    for copy in later:
-        copy.wait_recv()
-    clear_borders(1)
-    convolve(ratio_ref, 1, True)
+    receive(late_across)
+    clear_columns(1, (middle,), ROWS)
+    forward_inner(ratio_ref, 1)
+    receive(late_along)
+    receive(late_corners)
+    clear_rows(1)
+    forward_edge(1)
+    convolve(1, True)
     for group in (0, 1):
         at = pl.ds(4 * group, 4)
         updated = est_ref[at] * inverse(group)
@@ -474,19 +533,16 @@
     tile_ref[...] = placed[0:1] + pltpu.roll(placed[1:2], 4 * ny, 1)
     me = gx * ny + gy
 
-    def send(k, carry):
+    pl.semaphore_wait(widest_sem, len(widest))
+    for dx, dy in far:
         pltpu.make_async_remote_copy(
             src_ref=tile_ref,
             dst_ref=gathered.at[me],
             send_sem=all_send,
             recv_sem=all_recv,
-            device_id=device(*far(k)),
+            device_id=device(dx, dy),
             device_id_type=MESH,
         ).start()
-        return carry
-
-    pl.semaphore_wait(widest_sem, len(widest))
-    over_far(send)
     gathered[me] = tile_ref[...]
     others = gathered.at[pl.ds(0, count - 1)]
     everyone = pltpu.make_async_remote_copy(
@@ -502,7 +558,7 @@
     five_ref[0, pl.ds(0, nx, stride=2), :] = strips[:, : 4 * ny]
     five_ref[0, pl.ds(1, nx, stride=2), :] = pltpu.roll(strips, 128 - 4 * ny, 1)[:, : 4 * ny]
 
-    for copy in copies + later:
+    for copy in along + corners + across + late_along + late_corners + late_across:
         copy.wait_send()
     for turn in (0, 1):
         for z in range(8):
@@ -552,7 +608,7 @@
         + [
             pltpu.VMEM((32, 32, 128), F32),
             pltpu.VMEM((32, 32, 256), F32),
-            pltpu.VMEM((32, 2 * LX, 128), F32),
+            pltpu.VMEM((32, 3 * LX, 128), F32),
             pltpu.VMEM((8, ROWS, COLUMNS), F32),
             pltpu.VMEM((2, 2, 8, EDGE, 128), F32),
             pltpu.VMEM((2, 2, LX, 128), F32),
@@ -568,8 +624,8 @@
             pltpu.VMEM((1, 128), F32),
             pltpu.VMEM((nx * ny, 1, 128), F32),
             pltpu.SemaphoreType.DMA((len(kept),)),
-            pltpu.SemaphoreType.DMA((2, 8)),
-            pltpu.SemaphoreType.DMA((2, 8)),
+            pltpu.SemaphoreType.DMA((2, 10)),
+            pltpu.SemaphoreType.DMA((2, 10)),
             pltpu.SemaphoreType.DMA((2, 8)),
             pltpu.SemaphoreType.DMA((2, 8)),
             pltpu.SemaphoreType.DMA,

time: 43.4 us -> 40.6 us (0.935)
  Pallas kernels: 42 us -> 39.2 us
    pallas_call x1, Pallas kernels: 41.3 us -> 38.4 us  [local(): pl.pallas_call(functools.partial(body, nx, ny), out_shape=out_shape, in_s...]
where the time goes in v2:
time: 40.6 us; the launch traced here: 40.5 us
  Pallas kernels  39.2 us (97%)
  between operations  1.29 us (3%)
    pallas_call x1, Pallas kernels, local(): pl.pallas_call(functools.partial(body, nx, ny), out_shape=out_shape, in_s...  38.4 us

profile of v2, /device:TPU:1, one launch (start us, length us, event | category | flops | bytes accessed | tf_op | source)
XLA Modules:
  0.0 40.5 jit_solution(18378755521433088704)
XLA Ops:
  1.3 38.4 %shard_map.172 = (f32[8,64,128]{2,1,0:T(8,128)S(1)}, f32[4,32,64]{2,1,0:T(8,128)S(1)}, f32[2,16,32]{2,1,0:T(8,128)S(1)}, f32[1,8,16]{2,1,0:T(8,128)S(1)}, f32[1,...) custom-call(s32[1]{0:T(128)S(6)} %copy.19.index_ref, f32[8,64,128]{2,1,0:T(8,128)} %refs_0_.1, f32[8,64,128]{2,1,0:T(8,128)} %refs_1_.1, ...), custom_call_target="tpu_custom_call" | custom-call | tf_op jit(solution)/shard_map/pallas_call | solution.py:596
  39.7 0.8 %shard_map.173 = (f32[8,64,128]{2,1,0:T(8,128)}, f32[4,32,64]{2,1,0:T(8,128)}, f32[2,16,32]{2,1,0:T(8,128)}, f32[1,8,16]{2,1,0:T(8,128)}, f32[1,4,8]{2,1,0:T(4,128)}, /*index=5*/f32[1,32,32]{2,1,0:T(8,128)}) custom-call(f32[8,64,128]{2,1,0:T(8,128)S(1)} %get-tuple-element.12.refs_0_, f32[4,32,64]{2,1,0:T(8,128)S(1)} %get-tuple-element.13.refs_1_, ...), custom_call_target="tpu_custom_call" | custom-call | tf_op jit(solution)/shard_map/pallas_call | solution.py:642

commit v3 on v2

--- a/solution.py
+++ b/solution.py
@@ -53,8 +53,7 @@
     inner = column_table(EDGE + np.arange(COLUMNS))
     left = column_table(np.arange(EDGE))
     right = column_table(LY - EDGE + np.arange(EDGE))
-    first = stacked(np.concatenate([inner] + [left, right] * 4))
-    second = stacked(np.concatenate([inner] + [right, left] * 4))
+    columns = stacked(np.concatenate([inner] + [left, right] * 4))
     inner_rows = beside(row_table(EDGE + np.arange(ROWS)))
     edge_rows = beside(row_table(np.concatenate([np.arange(EDGE), LX - EDGE + np.arange(EDGE)])))
     angle = 2.0 * np.pi / LX * np.outer(EDGE + np.arange(ROWS), np.arange(LX))
@@ -81,8 +80,7 @@
             pools[column, 128 * level + column // step] = 1.0 / step
     pools = np.concatenate([pools] * 3, axis=0).astype(BF16)
     return (
-        first,
-        second,
+        columns,
         inner_rows,
         edge_rows,
         rows_back,
@@ -121,15 +119,14 @@
 
 
 def body(nx, ny, index_ref, *refs):
-    inputs, refs = refs[:12], refs[12:]
+    inputs, refs = refs[:11], refs[11:]
     updated_ref, one_ref, two_ref, three_ref, four_ref, five_ref = refs[:6]
-    held, refs = refs[6:18], refs[18:]
+    held, refs = refs[6:17], refs[17:]
     (
         est_ref,
         view_ref,
         psf_ref,
-        first_ref,
-        second_ref,
+        columns_ref,
         inner_rows_ref,
         edge_rows_ref,
         rows_back_ref,
@@ -165,6 +162,7 @@
         swap_recv,
         all_send,
         all_recv,
+        near_sem,
         wider_sem,
         widest_sem,
     ) = refs
@@ -198,7 +196,7 @@
     barrier = pltpu.get_barrier_semaphore()
     for peer in peers:
         pl.semaphore_signal(barrier, inc=1, device_id=device(*peer), device_id_type=MESH)
-    for k in (2, 9, 10, 3, 4, 5, 6, 7, 8, 1, 11):
+    for k in (2, 8, 9, 3, 4, 5, 6, 7, 1, 10):
         fetches[k].start()
 
     def spread_word(sem, offsets):
@@ -207,6 +205,7 @@
 
     wider = [(dx, dy) for dx in (-2, 0, 2) for dy in (-2, 0, 2) if (dx, dy) != (0, 0)]
     widest = [(-4, 0), (4, 0)]
+    close = [(dx, dy) for dx, dy, dz in peers if dz == 0]
 
     def pack(source, turn, group):
         lane = lax.broadcasted_iota(jnp.int32, (ROWS, 128), 1)
@@ -230,9 +229,25 @@
     middle, top, bottom = pl.ds(EDGE, ROWS), pl.ds(0, EDGE), pl.ds(EDGE + ROWS, EDGE)
     head, tail = pl.ds(0, EDGE), pl.ds(ROWS - EDGE, EDGE)
 
+    def there(dx, dy):
+        tests = []
+        if dx:
+            tests.append(gx > 0 if dx < 0 else gx < nx - 1)
+        if dy:
+            tests.append(gy > 0 if dy < 0 else gy < ny - 1)
+        return tests[0] if len(tests) == 1 else tests[0] & tests[1]
+
+    def send(copies):
+        for copy, ahead, _ in copies:
+            pl.when(ahead)(copy.start)
+
+    def receive(copies):
+        for copy, _, behind in copies:
+            pl.when(behind)(copy.wait_recv)
+
     def halo_copies(source, turn):
         def copy(src, dst, at, dx, dy):
-            return pltpu.make_async_remote_copy(
+            sent = pltpu.make_async_remote_copy(
                 src_ref=src,
                 dst_ref=dst,
                 send_sem=send_sem.at[turn, at],
@@ -240,6 +255,7 @@
                 device_id=device(dx, dy),
                 device_id_type=MESH,
             )
+            return sent, there(dx, dy), there(-dx, -dy)
 
         right, left = packed.at[turn, 0], packed.at[turn, 1]
         from_left, from_right = edge_columns.at[turn, 0], edge_columns.at[turn, 1]
@@ -261,31 +277,23 @@
         ]
         return along, corners, across
 
-    def clear_columns(turn, rows, height):
-        @pl.when(gy == 0)
-        def _():
-            for at in rows:
-                edge_columns[turn, 0, at, :] = jnp.zeros((height, 128), F32)
-
-        @pl.when(gy == ny - 1)
-        def _():
-            for at in rows:
-                edge_columns[turn, 1, at, :] = jnp.zeros((height, 128), F32)
-
-    def clear_rows(turn):
-        @pl.when(gx == 0)
-        def _():
-            edge_rows[turn, 0] = jnp.zeros((8, EDGE, 128), F32)
-            for side in (0, 1):
-                edge_columns[turn, side, top, :] = jnp.zeros((EDGE, 128), F32)
-
-        @pl.when(gx == nx - 1)
-        def _():
-            edge_rows[turn, 1] = jnp.zeros((8, EDGE, 128), F32)
-            for side in (0, 1):
-                edge_columns[turn, side, bottom, :] = jnp.zeros((EDGE, 128), F32)
-
-        clear_columns(turn, (top, bottom), EDGE)
+    def clear_borders():
+        rows, columns = jnp.zeros((8, EDGE, 128), F32), jnp.zeros((LX, 128), F32)
+        for end, at, part in ((gx == 0, 0, top), (gx == nx - 1, 1, bottom)):
+
+            @pl.when(end)
+            def _():
+                for turn in (0, 1):
+                    edge_rows[turn, at] = rows
+                    for side in (0, 1):
+                        edge_columns[turn, side, part, :] = columns[:EDGE]
+
+        for end, side in ((gy == 0, 0), (gy == ny - 1, 1)):
+
+            @pl.when(end)
+            def _():
+                for turn in (0, 1):
+                    edge_columns[turn, side] = columns
 
     def partner_copy(turn, z):
         return pltpu.make_async_remote_copy(
@@ -300,16 +308,21 @@
     def transform(turn, height, plane_of, left, right, rows_table, adding):
         lane = lax.broadcasted_iota(jnp.int32, (height, 128), 1)
         even = (lane & EDGE) == 0
-        for group, table in ((0, first_ref), (1, second_ref)):
-            mixed = jnp.where(even, left, right) if group == 0 else jnp.where(even, right, left)
-            rows = []
-            for j in range(4):
-                side = jnp.where((lane >= 32 * j) & (lane < 32 * j + 32), mixed, 0.0)
-                rows.append(jnp.concatenate([plane_of(4 * group + j), side], axis=1))
-            half = dot(left_triple(jnp.concatenate(rows, axis=0)), table[...])
+        mixed = (
+            jnp.where(even, left, right),
+            jnp.where(even, pltpu.roll(left, 128 - EDGE, 1), pltpu.roll(right, EDGE, 1)),
+        )
+        rows = []
+        for z in range(8):
+            j = 32 * (z % 4)
+            side = jnp.where((lane >= j) & (lane < j + 32), mixed[z // 4], 0.0)
+            rows.append(jnp.concatenate([plane_of(z), side], axis=1))
+        half = dot(left_triple(jnp.concatenate(rows, axis=0)), columns_ref[...])
+        for group in (0, 1):
             for pair in (0, 1):
-                a = half[2 * pair * height : (2 * pair + 1) * height]
-                b = half[(2 * pair + 1) * height : (2 * pair + 2) * height]
+                z = 4 * group + 2 * pair
+                a = half[z * height : (z + 1) * height]
+                b = half[(z + 1) * height : (z + 2) * height]
                 joint = jnp.concatenate(
                     [
                         jnp.concatenate([a[:, :128], b[:, :128]], axis=1),
@@ -318,7 +331,6 @@
                     axis=0,
                 )
                 full = dot(rows_table[...], right_triple(joint))
-                z = 4 * group + 2 * pair
                 for b in (0, 1):
                     part = full[:, 128 * b : 128 * b + 128]
                     if adding:
@@ -346,7 +358,12 @@
         transform(turn, 2 * EDGE, plane_of, left, right, edge_rows_ref, True)
 
     def depth(x_ref, turn, base, mirrored, adding):
-        def block(step, carry):
+        def blocks(step, carry):
+            block(2 * step)
+            block(2 * step + 1)
+            return carry
+
+        def block(step):
             at = pl.multiple_of(step * 8, 8)
             re, im = pl.ds(at, 8), pl.ds(pl.multiple_of(at + LX, 8), 8)
             xr = [x_ref[turn, z, re, :] for z in range(8)]
@@ -377,21 +394,19 @@
             for z in range(8):
                 product_ref[z, re, :] = yr[z]
                 product_ref[z, im, :] = yi[z]
-            return carry
-
-        lax.fori_loop(0, LX // 8, block, 0)
-
-    def inverse(group):
+
+        lax.fori_loop(0, LX // 16, blocks, 0)
+
+    def inverse(planes):
         rows = []
-        for pair in (0, 1):
-            z = 4 * group + 2 * pair
+        for z in planes[::2]:
             joint = jnp.concatenate([product_ref[z], product_ref[z + 1]], axis=1)
             half = dot(rows_back_ref[...], right_triple(joint))
             for b in (0, 1):
                 lanes = slice(128 * b, 128 * b + 128)
                 rows.append(jnp.concatenate([half[:ROWS, lanes], half[ROWS:, lanes]], axis=1))
         full = dot(jnp.concatenate(two(jnp.concatenate(rows, axis=0)), axis=1), columns_back_ref[...])
-        return (full[:, :COLUMNS] + full[:, COLUMNS:]).reshape(4, ROWS, COLUMNS)
+        return (full[:, :COLUMNS] + full[:, COLUMNS:]).reshape(len(planes), ROWS, COLUMNS)
 
     def convolve(turn, mirrored):
         depth(own_ref, turn, HALO, mirrored, False)
@@ -401,7 +416,7 @@
         depth(other_ref, turn, base, mirrored, True)
 
     def spectrum():
-        for k in (2, 9, 10):
+        for k in (2, 8, 9):
             fetches[k].wait()
         view = index_ref[0]
         taps_ref[...] = jnp.zeros((32, 32, 128), F32)
@@ -444,48 +459,41 @@
     pack(est_ref, 0, 0)
     pack(est_ref, 0, 1)
     pl.semaphore_wait(barrier, len(peers))
+    spread_word(near_sem, close)
     along, corners, across = halo_copies(est_ref, 0)
-    for copy in along + corners + across:
-        copy.start()
+    send(corners + across + along)
+    clear_borders()
     spectrum()
-    for k in (3, 4, 5, 6, 7, 8, 1, 11):
+    for k in (3, 4, 5, 6, 7, 1, 10):
         fetches[k].wait()
-
-    def receive(copies):
-        for copy in copies:
-            copy.wait_recv()
-
     receive(across)
-    clear_columns(0, (middle,), ROWS)
     forward_inner(est_ref, 0)
-    receive(along)
-    receive(corners)
+    pl.semaphore_wait(near_sem, len(close))
     spread_word(wider_sem, wider)
-    clear_rows(0)
+    receive(along + corners)
     forward_edge(0)
     convolve(0, False)
     late_along, late_corners, late_across = halo_copies(ratio_ref, 1)
     for group in (0, 1):
         at = pl.ds(4 * group, 4)
-        ratio_ref[at] = view_ref[at] / inverse(group)
-        for copy in late_along[2 * group : 2 * group + 2]:
-            copy.start()
-        pack(ratio_ref, 1, group)
-    for copy in late_corners + late_across:
-        copy.start()
+        ratio_ref[at] = view_ref[at] / inverse(range(4 * group, 4 * group + 4))
+        if group == 1:
+            pack(ratio_ref, 1, 1)
+            send(late_corners + late_across)
+        send(late_along[2 * group : 2 * group + 2])
+        if group == 0:
+            pack(ratio_ref, 1, 0)
     pl.semaphore_wait(wider_sem, len(wider))
     spread_word(widest_sem, widest)
     receive(late_across)
-    clear_columns(1, (middle,), ROWS)
     forward_inner(ratio_ref, 1)
-    receive(late_along)
-    receive(late_corners)
-    clear_rows(1)
+    receive(late_along + late_corners)
     forward_edge(1)
     convolve(1, True)
+    correction = inverse(range(8))
     for group in (0, 1):
         at = pl.ds(4 * group, 4)
-        updated = est_ref[at] * inverse(group)
+        updated = est_ref[at] * correction[4 * group : 4 * group + 4]
         updated_ref[at] = updated
         for pair in (0, 1):
             pool_a[2 * group + pair] = updated[2 * pair] + updated[2 * pair + 1]
@@ -558,8 +566,8 @@
     five_ref[0, pl.ds(0, nx, stride=2), :] = strips[:, : 4 * ny]
     five_ref[0, pl.ds(1, nx, stride=2), :] = pltpu.roll(strips, 128 - 4 * ny, 1)[:, : 4 * ny]
 
-    for copy in along + corners + across + late_along + late_corners + late_across:
-        copy.wait_send()
+    for copy, ahead, _ in along + corners + across + late_along + late_corners + late_across:
+        pl.when(ahead)(copy.wait_send)
     for turn in (0, 1):
         for z in range(8):
             partner_copy(turn, z).wait_send()
@@ -634,6 +642,7 @@
             pltpu.SemaphoreType.DMA,
             pltpu.SemaphoreType.REGULAR,
             pltpu.SemaphoreType.REGULAR,
+            pltpu.SemaphoreType.REGULAR,
         ],
         compiler_params=pltpu.CompilerParams(
             collective_id=0, has_side_effects=True, vmem_limit_bytes=32 << 20

time: 40.6 us -> 39.1 us (0.963)
  Pallas kernels: 39.2 us -> 37.8 us
    pallas_call x1, Pallas kernels: 38.4 us -> 37 us  [local(): pl.pallas_call(functools.partial(body, nx, ny), out_shape=out_shape, in_s...]
where the time goes in v3:
time: 39.1 us; the launch traced here: 39 us
  Pallas kernels  37.8 us (97%)
  between operations  1.29 us (3%)
    pallas_call x1, Pallas kernels, local(): pl.pallas_call(functools.partial(body, nx, ny), out_shape=out_shape, in_s...  37 us
    pallas_call x1, Pallas kernels, local(): pl.pallas_call(hand_over, out_shape=out_shape, in_specs=[vmem] * 6, out_s...  0.78 us

profile of v3, /device:TPU:1, one launch (start us, length us, event | category | flops | bytes accessed | tf_op | source)
XLA Modules:
  0.0 39.0 jit_solution(6797041885327932115)
XLA Ops:
  1.3 37.0 %shard_map.163 = (f32[8,64,128]{2,1,0:T(8,128)S(1)}, f32[4,32,64]{2,1,0:T(8,128)S(1)}, f32[2,16,32]{2,1,0:T(8,128)S(1)}, f32[1,8,16]{2,1,0:T(8,128)S(1)}, f32[1,...) custom-call(s32[1]{0:T(128)S(6)} %copy.18.index_ref, f32[8,64,128]{2,1,0:T(8,128)} %refs_0_.1, f32[8,64,128]{2,1,0:T(8,128)} %refs_1_.1, ...), custom_call_target="tpu_custom_call" | custom-call | tf_op jit(solution)/shard_map/pallas_call | solution.py:604
  38.3 0.8 %shard_map.164 = (f32[8,64,128]{2,1,0:T(8,128)}, f32[4,32,64]{2,1,0:T(8,128)}, f32[2,16,32]{2,1,0:T(8,128)}, f32[1,8,16]{2,1,0:T(8,128)}, f32[1,4,8]{2,1,0:T(4,128)}, /*index=5*/f32[1,32,32]{2,1,0:T(8,128)}) custom-call(f32[8,64,128]{2,1,0:T(8,128)S(1)} %get-tuple-element.12.refs_0_, f32[4,32,64]{2,1,0:T(8,128)S(1)} %get-tuple-element.13.refs_1_, ...), custom_call_target="tpu_custom_call" | custom-call | tf_op jit(solution)/shard_map/pallas_call | solution.py:651

commit v4 on v3

--- a/solution.py
+++ b/solution.py
@@ -79,16 +79,13 @@
         for column in range(COLUMNS):
             pools[column, 128 * level + column // step] = 1.0 / step
     pools = np.concatenate([pools] * 3, axis=0).astype(BF16)
-    return (
-        columns,
-        inner_rows,
-        edge_rows,
-        rows_back,
-        columns_back,
-        tap_columns,
-        tap_rows,
-        pools,
-    )
+    tall = np.concatenate([columns, columns_back, tap_columns, pools[:, :256], pools[:, 256:]])
+    wide = np.zeros((2 * LX, 1536), BF16)
+    wide[:, :384] = inner_rows
+    wide[:, 384:576] = edge_rows
+    wide[:, 640:832] = tap_rows
+    wide[: 2 * ROWS, 896:1472] = rows_back
+    return tall, wide
 
 
 def two(x):
@@ -119,22 +116,10 @@
 
 
 def body(nx, ny, index_ref, *refs):
-    inputs, refs = refs[:11], refs[11:]
+    inputs, refs = refs[:5], refs[5:]
     updated_ref, one_ref, two_ref, three_ref, four_ref, five_ref = refs[:6]
-    held, refs = refs[6:17], refs[17:]
-    (
-        est_ref,
-        view_ref,
-        psf_ref,
-        columns_ref,
-        inner_rows_ref,
-        edge_rows_ref,
-        rows_back_ref,
-        columns_back_ref,
-        tap_columns_ref,
-        tap_rows_ref,
-        pools_ref,
-    ) = held
+    held, refs = refs[6:11], refs[11:]
+    est_ref, view_ref, psf_ref, tall_ref, wide_ref = held
     (
         taps_ref,
         tap_half_ref,
@@ -162,9 +147,8 @@
         swap_recv,
         all_send,
         all_recv,
-        near_sem,
-        wider_sem,
-        widest_sem,
+        word_sem,
+        pair_sem,
     ) = refs
     gx, gy, gz = lax.axis_index("gx"), lax.axis_index("gy"), lax.axis_index("gz")
 
@@ -183,29 +167,51 @@
     ]
     fetches[0].start()
 
-    peers = [(dx, dy, 0) for dx in (-1, 0, 1) for dy in (-1, 0, 1) if (dx, dy) != (0, 0)]
-    peers.append((0, 0, 1))
     count = nx * ny
 
+    def there(dx, dy):
+        tests = []
+        if dx:
+            tests.append(gx >= -dx if dx < 0 else gx < nx - dx)
+        if dy:
+            tests.append(gy >= -dy if dy < 0 else gy < ny - dy)
+        return tests[0] if len(tests) == 1 else tests[0] & tests[1]
+
+    def box(reach):
+        steps = (-reach, 0, reach)
+        return [(dx, dy) for dx in steps for dy in steps if (dx, dy) != (0, 0)]
+
     def hops(offset):
-        dx, dy = offset
+        dx, dy, dz = offset
         ring = lambda k, n: min(k, n - k)
-        return ring(dx % 4, 4) + ring(dx // 4, nx // 4) + ring(dy, ny)
-
-    far = sorted(((dx, dy) for dx in range(nx) for dy in range(ny)), key=hops, reverse=True)[:-1]
+        return ring(dx % 4, 4) + ring(dx // 4, nx // 4) + ring(dy, ny) + 0.5 * dz
+
+    every = ((dx, dy, dz) for dx in range(nx) for dy in range(ny) for dz in (0, 1))
+    far = sorted(every, key=hops, reverse=True)[:-1]
+
+    def signal_all(sem, offsets):
+        for dx, dy in offsets:
+
+            @pl.when(there(dx, dy))
+            def _():
+                pl.semaphore_signal(sem, inc=1, device_id=device(dx, dy), device_id_type=MESH)
+
+    def number(offsets):
+        return sum(jnp.where(there(dx, dy), 1, 0) for dx, dy in offsets)
+
+    rounds = [box(1), box(2), box(4), [(-8, 0), (8, 0)]]
+
+    def spread_word(k):
+        signal_all(word_sem.at[k], rounds[k])
+
+    def hear_word(k):
+        pl.semaphore_wait(word_sem.at[k], number(rounds[k]))
+
     barrier = pltpu.get_barrier_semaphore()
-    for peer in peers:
-        pl.semaphore_signal(barrier, inc=1, device_id=device(*peer), device_id_type=MESH)
-    for k in (2, 8, 9, 3, 4, 5, 6, 7, 1, 10):
+    pl.semaphore_signal(barrier, inc=1, device_id=device(0, 0, 1), device_id_type=MESH)
+    signal_all(barrier, box(1))
+    for k in (4, 3, 2, 1):
         fetches[k].start()
-
-    def spread_word(sem, offsets):
-        for dx, dy in offsets:
-            pl.semaphore_signal(sem, inc=1, device_id=device(dx, dy), device_id_type=MESH)
-
-    wider = [(dx, dy) for dx in (-2, 0, 2) for dy in (-2, 0, 2) if (dx, dy) != (0, 0)]
-    widest = [(-4, 0), (4, 0)]
-    close = [(dx, dy) for dx, dy, dz in peers if dz == 0]
 
     def pack(source, turn, group):
         lane = lax.broadcasted_iota(jnp.int32, (ROWS, 128), 1)
@@ -229,33 +235,48 @@
     middle, top, bottom = pl.ds(EDGE, ROWS), pl.ds(0, EDGE), pl.ds(EDGE + ROWS, EDGE)
     head, tail = pl.ds(0, EDGE), pl.ds(ROWS - EDGE, EDGE)
 
-    def there(dx, dy):
-        tests = []
-        if dx:
-            tests.append(gx > 0 if dx < 0 else gx < nx - 1)
-        if dy:
-            tests.append(gy > 0 if dy < 0 else gy < ny - 1)
-        return tests[0] if len(tests) == 1 else tests[0] & tests[1]
-
     def send(copies):
-        for copy, ahead, _ in copies:
+        for copy, ahead in copies:
             pl.when(ahead)(copy.start)
 
-    def receive(copies):
-        for copy, _, behind in copies:
-            pl.when(behind)(copy.wait_recv)
+    def wait_units(sem, units, send):
+        for last_x in (True, False):
+            for last_y in (True, False):
+                end_x = (gx == 0) | (gx == nx - 1)
+                end_y = (gy == 0) | (gy == ny - 1)
+                here = (end_x if last_x else ~end_x) & (end_y if last_y else ~end_y)
+                total = units(1 if last_x else 2, 1 if last_y else 2)
+                slab = kernel_ref.at[pl.ds(0, 2), pl.ds(0, total * EDGE // 2)]
+                copy = pltpu.make_async_remote_copy(
+                    src_ref=slab,
+                    dst_ref=slab,
+                    send_sem=sem,
+                    recv_sem=sem,
+                    device_id=device(0, 0, 1),
+                    device_id_type=MESH,
+                )
+                pl.when(here)(copy.wait_send if send else copy.wait_recv)
+
+    def receive_strips(turn):
+        wait_units(recv_sem.at[turn, 1], lambda sx, sy: 4 * sy, False)
+
+    def receive_edges(turn):
+        wait_units(recv_sem.at[turn, 0], lambda sx, sy: sx * (8 + sy), False)
+
+    def finish_sends(turn):
+        wait_units(send_sem.at[turn], lambda sx, sy: 4 * sy + sx * (8 + sy), True)
 
     def halo_copies(source, turn):
         def copy(src, dst, at, dx, dy):
             sent = pltpu.make_async_remote_copy(
                 src_ref=src,
                 dst_ref=dst,
-                send_sem=send_sem.at[turn, at],
+                send_sem=send_sem.at[turn],
                 recv_sem=recv_sem.at[turn, at],
                 device_id=device(dx, dy),
                 device_id_type=MESH,
             )
-            return sent, there(dx, dy), there(-dx, -dy)
+            return sent, there(dx, dy)
 
         right, left = packed.at[turn, 0], packed.at[turn, 1]
         from_left, from_right = edge_columns.at[turn, 0], edge_columns.at[turn, 1]
@@ -263,17 +284,17 @@
         for group in (0, 1):
             planes = pl.ds(4 * group, 4)
             into = edge_rows.at[turn, 0, planes], edge_rows.at[turn, 1, planes]
-            along.append(copy(source.at[planes, tail, :], into[0], 2 * group, 1, 0))
-            along.append(copy(source.at[planes, head, :], into[1], 2 * group + 1, -1, 0))
+            along.append(copy(source.at[planes, tail, :], into[0], 0, 1, 0))
+            along.append(copy(source.at[planes, head, :], into[1], 0, -1, 0))
         corners = [
-            copy(right.at[tail, :], from_left.at[top, :], 4, 1, 1),
-            copy(right.at[head, :], from_left.at[bottom, :], 5, -1, 1),
-            copy(left.at[tail, :], from_right.at[top, :], 6, 1, -1),
-            copy(left.at[head, :], from_right.at[bottom, :], 7, -1, -1),
+            copy(right.at[tail, :], from_left.at[top, :], 0, 1, 1),
+            copy(right.at[head, :], from_left.at[bottom, :], 0, -1, 1),
+            copy(left.at[tail, :], from_right.at[top, :], 0, 1, -1),
+            copy(left.at[head, :], from_right.at[bottom, :], 0, -1, -1),
         ]
         across = [
-            copy(right, from_left.at[middle, :], 8, 0, 1),
-            copy(left, from_right.at[middle, :], 9, 0, -1),
+            copy(right, from_left.at[middle, :], 1, 0, 1),
+            copy(left, from_right.at[middle, :], 1, 0, -1),
         ]
         return along, corners, across
 
@@ -299,8 +320,8 @@
         return pltpu.make_async_remote_copy(
             src_ref=own_ref.at[turn, z],
             dst_ref=other_ref.at[turn, z],
-            send_sem=part_send.at[turn, z],
-            recv_sem=part_recv.at[turn, z],
+            send_sem=part_send,
+            recv_sem=part_recv.at[turn],
             device_id=device(0, 0, 1),
             device_id_type=MESH,
         )
@@ -317,7 +338,7 @@
             j = 32 * (z % 4)
             side = jnp.where((lane >= j) & (lane < j + 32), mixed[z // 4], 0.0)
             rows.append(jnp.concatenate([plane_of(z), side], axis=1))
-        half = dot(left_triple(jnp.concatenate(rows, axis=0)), columns_ref[...])
+        half = dot(left_triple(jnp.concatenate(rows, axis=0)), tall_ref[0:768, :])
         for group in (0, 1):
             for pair in (0, 1):
                 z = 4 * group + 2 * pair
@@ -330,7 +351,7 @@
                     ],
                     axis=0,
                 )
-                full = dot(rows_table[...], right_triple(joint))
+                full = dot(wide_ref[:, rows_table], right_triple(joint))
                 for b in (0, 1):
                     part = full[:, 128 * b : 128 * b + 128]
                     if adding:
@@ -341,7 +362,7 @@
 
     def forward_inner(source, turn):
         left, right = edge_columns[turn, 0, middle, :], edge_columns[turn, 1, middle, :]
-        transform(turn, ROWS, lambda z: source[z], left, right, inner_rows_ref, False)
+        transform(turn, ROWS, lambda z: source[z], left, right, slice(0, 384), False)
 
     def forward_edge(turn):
         def both(a, b):
@@ -355,7 +376,7 @@
         def plane_of(z):
             return both(edge_rows[turn, 0, z], edge_rows[turn, 1, z])
 
-        transform(turn, 2 * EDGE, plane_of, left, right, edge_rows_ref, True)
+        transform(turn, 2 * EDGE, plane_of, left, right, slice(384, 576), True)
 
     def depth(x_ref, turn, base, mirrored, adding):
         def blocks(step, carry):
@@ -401,22 +422,30 @@
         rows = []
         for z in planes[::2]:
             joint = jnp.concatenate([product_ref[z], product_ref[z + 1]], axis=1)
-            half = dot(rows_back_ref[...], right_triple(joint))
+            half = dot(wide_ref[0:128, 896:1472], right_triple(joint))
             for b in (0, 1):
                 lanes = slice(128 * b, 128 * b + 128)
                 rows.append(jnp.concatenate([half[:ROWS, lanes], half[ROWS:, lanes]], axis=1))
-        full = dot(jnp.concatenate(two(jnp.concatenate(rows, axis=0)), axis=1), columns_back_ref[...])
+        full = dot(jnp.concatenate(two(jnp.concatenate(rows, axis=0)), axis=1), tall_ref[768:1280, :])
         return (full[:, :COLUMNS] + full[:, COLUMNS:]).reshape(len(planes), ROWS, COLUMNS)
 
-    def convolve(turn, mirrored):
+    def convolve(turn, mirrored, between):
         depth(own_ref, turn, HALO, mirrored, False)
-        for z in range(8):
-            partner_copy(turn, z).wait_recv()
+        between()
+        planes = other_ref.at[turn]
+        pltpu.make_async_remote_copy(
+            src_ref=planes,
+            dst_ref=planes,
+            send_sem=part_send,
+            recv_sem=part_recv.at[turn],
+            device_id=device(0, 0, 1),
+            device_id_type=MESH,
+        ).wait_recv()
         base = HALO + 8 - 16 * gz if mirrored else HALO - 8 + 16 * gz
         depth(other_ref, turn, base, mirrored, True)
 
     def spectrum():
-        for k in (2, 8, 9):
+        for k in (4, 3, 2):
             fetches[k].wait()
         view = index_ref[0]
         taps_ref[...] = jnp.zeros((32, 32, 128), F32)
@@ -430,7 +459,7 @@
             high = x.astype(BF16).astype(F32)
             low = x - high
             joint = high + pltpu.roll(high, 32, 1) + pltpu.roll(low, 64, 1)
-            half = dot(joint.astype(BF16), tap_columns_ref[...])
+            half = dot(joint.astype(BF16), tall_ref[1280:1408, :])
             tap_half_ref[8 * step : 8 * step + 8] = half.reshape(8, 32, 256)
 
         def rows(step, carry):
@@ -444,7 +473,7 @@
                     ],
                     axis=0,
                 )
-                full = dot(tap_rows_ref[...], right_triple(joint))
+                full = dot(wide_ref[:, 640:832], right_triple(joint))
                 for b in (0, 1):
                     re = full[:LX, 128 * b : 128 * b + 128]
                     im = full[LX:, 128 * b : 128 * b + 128]
@@ -458,21 +487,20 @@
     fetches[0].wait()
     pack(est_ref, 0, 0)
     pack(est_ref, 0, 1)
-    pl.semaphore_wait(barrier, len(peers))
-    spread_word(near_sem, close)
+    pl.semaphore_wait(barrier, 1 + number(box(1)))
+    spread_word(0)
     along, corners, across = halo_copies(est_ref, 0)
     send(corners + across + along)
     clear_borders()
     spectrum()
-    for k in (3, 4, 5, 6, 7, 1, 10):
-        fetches[k].wait()
-    receive(across)
+    fetches[1].wait()
+    receive_strips(0)
     forward_inner(est_ref, 0)
-    pl.semaphore_wait(near_sem, len(close))
-    spread_word(wider_sem, wider)
-    receive(along + corners)
+    receive_edges(0)
     forward_edge(0)
-    convolve(0, False)
+    hear_word(0)
+    spread_word(1)
+    convolve(0, False, lambda: None)
     late_along, late_corners, late_across = halo_copies(ratio_ref, 1)
     for group in (0, 1):
         at = pl.ds(4 * group, 4)
@@ -483,21 +511,45 @@
         send(late_along[2 * group : 2 * group + 2])
         if group == 0:
             pack(ratio_ref, 1, 0)
-    pl.semaphore_wait(wider_sem, len(wider))
-    spread_word(widest_sem, widest)
-    receive(late_across)
+    hear_word(1)
+    spread_word(2)
+    receive_strips(1)
     forward_inner(ratio_ref, 1)
-    receive(late_along + late_corners)
+    receive_edges(1)
     forward_edge(1)
-    convolve(1, True)
-    correction = inverse(range(8))
-    for group in (0, 1):
-        at = pl.ds(4 * group, 4)
-        updated = est_ref[at] * correction[4 * group : 4 * group + 4]
-        updated_ref[at] = updated
-        for pair in (0, 1):
-            pool_a[2 * group + pair] = updated[2 * pair] + updated[2 * pair + 1]
-
+    hear_word(2)
+    spread_word(3)
+
+    def tell_partner():
+        hear_word(3)
+        pl.semaphore_signal(pair_sem, inc=1, device_id=device(0, 0, 1), device_id_type=MESH)
+
+    convolve(1, True, tell_partner)
+    updated = est_ref[...] * inverse(range(8))
+    column_sums = jnp.sum(updated, axis=0)
+    halves = [jnp.sum(column_sums[32 * i : 32 * i + 32], axis=0, keepdims=True) for i in (0, 1)]
+    source = lax.broadcasted_iota(jnp.int32, (384, 128), 0) % 128
+    target = lax.broadcasted_iota(jnp.int32, (384, 128), 1)
+    place = jnp.where(target == 4 * gy + source // 32, 2.0**-14, 0.0).astype(BF16)
+    eight = jnp.concatenate(halves + [jnp.zeros((6, 128), F32)], axis=0)
+    placed = dot(exact_triple(eight), place)
+    tile_ref[...] = placed[0:1] + pltpu.roll(placed[1:2], 4 * ny, 1)
+    me = gz * count + gx * ny + gy
+    pl.semaphore_wait(pair_sem, 1)
+    for dx, dy, dz in far:
+        pltpu.make_async_remote_copy(
+            src_ref=tile_ref,
+            dst_ref=gathered.at[me],
+            send_sem=all_send,
+            recv_sem=all_recv,
+            device_id=device(dx, dy, dz),
+            device_id_type=MESH,
+        ).start()
+    gathered[me] = tile_ref[...]
+
+    updated_ref[...] = updated
+    for k in range(4):
+        pool_a[k] = updated[2 * k] + updated[2 * k + 1]
     even, odd = pl.ds(0, ROWS // 2, stride=2), pl.ds(1, ROWS // 2, stride=2)
     level_one = [(pool_a[k, even, :] + pool_a[k, odd, :]) * 0.25 for k in range(4)]
     for k in (0, 1):
@@ -511,7 +563,7 @@
     pool_d[8:16] = jnp.zeros((8, 128), F32)
     even, odd = pl.ds(0, 8, stride=2), pl.ds(1, 8, stride=2)
     level_four = (pool_d[even, :] + pool_d[odd, :]) * 0.5
-    plane_ref[0] = dot(exact_triple(level_four), pools_ref[:, 384:])
+    plane_ref[0] = dot(exact_triple(level_four), tall_ref[1792:2176, 128:256])
     swap = pltpu.make_async_remote_copy(
         src_ref=plane_ref.at[0],
         dst_ref=plane_ref.at[1],
@@ -521,58 +573,43 @@
         device_id_type=MESH,
     )
     swap.start()
-    third = dot(exact_triple(level_three), pools_ref[:, 256:384])
+    third = dot(exact_triple(level_three), tall_ref[1792:2176, 0:128])
     three_ref[0] = third[:, :16]
-    second = dot(exact_triple(jnp.concatenate(level_two, axis=0)), pools_ref[:, 128:256])
+    second = dot(exact_triple(jnp.concatenate(level_two, axis=0)), tall_ref[1408:1792, 128:256])
     for k in (0, 1):
         two_ref[k] = second[16 * k : 16 * k + 16, :32]
-    full = dot(exact_triple(jnp.concatenate(level_one, axis=0)), pools_ref[:, :128])
+    full = dot(exact_triple(jnp.concatenate(level_one, axis=0)), tall_ref[1408:1792, 0:128])
     for k in range(4):
         one_ref[k] = full[32 * k : 32 * k + 32, :64]
     swap.wait_recv()
     fourth = (plane_ref[0] + plane_ref[1]) * 0.5
     four_ref[0] = fourth[:4, :8]
-    pool_d[0:8] = fourth
-    fifth = pool_d[even, :] + pool_d[odd, :]
-    source = lax.broadcasted_iota(jnp.int32, (384, 128), 0) % 128
-    target = lax.broadcasted_iota(jnp.int32, (384, 128), 1)
-    place = (source < 8) & (target == 4 * gy + source // 2)
-    placed = dot(exact_triple(fifth), jnp.where(place, 0.25, 0.0).astype(BF16))
-    tile_ref[...] = placed[0:1] + pltpu.roll(placed[1:2], 4 * ny, 1)
-    me = gx * ny + gy
-
-    pl.semaphore_wait(widest_sem, len(widest))
-    for dx, dy in far:
-        pltpu.make_async_remote_copy(
-            src_ref=tile_ref,
-            dst_ref=gathered.at[me],
-            send_sem=all_send,
-            recv_sem=all_recv,
-            device_id=device(dx, dy),
-            device_id_type=MESH,
-        ).start()
-    gathered[me] = tile_ref[...]
-    others = gathered.at[pl.ds(0, count - 1)]
+
+    finish_sends(0)
+    finish_sends(1)
+    swap.wait_send()
+    pltpu.make_async_remote_copy(
+        src_ref=own_ref,
+        dst_ref=own_ref,
+        send_sem=part_send,
+        recv_sem=part_send,
+        device_id=device(0, 0, 1),
+        device_id_type=MESH,
+    ).wait_send()
+    others = gathered.at[pl.ds(0, 2 * count - 1)]
     everyone = pltpu.make_async_remote_copy(
         src_ref=others,
         dst_ref=others,
         send_sem=all_send,
         recv_sem=all_recv,
-        device_id=device(0, 1),
+        device_id=device(0, 0, 1),
         device_id_type=MESH,
     )
+    everyone.wait_send()
     everyone.wait_recv()
-    strips = jnp.sum(gathered[...].reshape(nx, ny, 128), axis=1)
+    strips = jnp.sum(gathered[...].reshape(2, nx, ny, 128), axis=(0, 2))
     five_ref[0, pl.ds(0, nx, stride=2), :] = strips[:, : 4 * ny]
     five_ref[0, pl.ds(1, nx, stride=2), :] = pltpu.roll(strips, 128 - 4 * ny, 1)[:, : 4 * ny]
-
-    for copy, ahead, _ in along + corners + across + late_along + late_corners + late_across:
-        pl.when(ahead)(copy.wait_send)
-    for turn in (0, 1):
-        for z in range(8):
-            partner_copy(turn, z).wait_send()
-    swap.wait_send()
-    everyone.wait_send()
 
 
 def hand_over(*refs):
@@ -630,18 +667,17 @@
             pltpu.VMEM((16, 128), F32),
             pltpu.VMEM((2, 8, 128), F32),
             pltpu.VMEM((1, 128), F32),
-            pltpu.VMEM((nx * ny, 1, 128), F32),
+            pltpu.VMEM((2 * nx * ny, 1, 128), F32),
             pltpu.SemaphoreType.DMA((len(kept),)),
-            pltpu.SemaphoreType.DMA((2, 10)),
-            pltpu.SemaphoreType.DMA((2, 10)),
-            pltpu.SemaphoreType.DMA((2, 8)),
-            pltpu.SemaphoreType.DMA((2, 8)),
+            pltpu.SemaphoreType.DMA((2,)),
+            pltpu.SemaphoreType.DMA((2, 2)),
+            pltpu.SemaphoreType.DMA,
+            pltpu.SemaphoreType.DMA((2,)),
             pltpu.SemaphoreType.DMA,
             pltpu.SemaphoreType.DMA,
             pltpu.SemaphoreType.DMA,
             pltpu.SemaphoreType.DMA,
-            pltpu.SemaphoreType.REGULAR,
-            pltpu.SemaphoreType.REGULAR,
+            pltpu.SemaphoreType.REGULAR((4,)),
             pltpu.SemaphoreType.REGULAR,
         ],
         compiler_params=pltpu.CompilerParams(

time: 39.1 us -> 38.2 us (0.977)
  Pallas kernels: 37.8 us -> 36.8 us
    pallas_call x1, Pallas kernels: 37 us -> 36 us  [local(): pl.pallas_call(functools.partial(body, nx, ny), out_shape=out_shape, in_s...]
where the time goes in v4:
time: 38.2 us; the launch traced here: 38.1 us
  Pallas kernels  36.8 us (96%)
  between operations  1.29 us (3%)
    pallas_call x1, Pallas kernels, local(): pl.pallas_call(functools.partial(body, nx, ny), out_shape=out_shape, in_s...  36 us
    pallas_call x1, Pallas kernels, local(): pl.pallas_call(hand_over, out_shape=out_shape, in_specs=[vmem] * 6, out_s...  0.78 us

profile of v4, /device:TPU:1, one launch (start us, length us, event | category | flops | bytes accessed | tf_op | source)
XLA Modules:
  0.0 38.1 jit_solution(3558206757110180671)
XLA Ops:
  1.3 36.0 %shard_map.109 = (f32[8,64,128]{2,1,0:T(8,128)S(1)}, f32[4,32,64]{2,1,0:T(8,128)S(1)}, f32[2,16,32]{2,1,0:T(8,128)S(1)}, f32[1,8,16]{2,1,0:T(8,128)S(1)}, f32[1,...) custom-call(s32[1]{0:T(128)S(6)} %copy.12.index_ref, f32[8,64,128]{2,1,0:T(8,128)} %refs_0_.1, f32[8,64,128]{2,1,0:T(8,128)} %refs_1_.1, ...), custom_call_target="tpu_custom_call" | custom-call | tf_op jit(solution)/shard_map/pallas_call | solution.py:641
  37.3 0.8 %shard_map.110 = (f32[8,64,128]{2,1,0:T(8,128)}, f32[4,32,64]{2,1,0:T(8,128)}, f32[2,16,32]{2,1,0:T(8,128)}, f32[1,8,16]{2,1,0:T(8,128)}, f32[1,4,8]{2,1,0:T(4,128)}, /*index=5*/f32[1,32,32]{2,1,0:T(8,128)}) custom-call(f32[8,64,128]{2,1,0:T(8,128)S(1)} %get-tuple-element.12.refs_0_, f32[4,32,64]{2,1,0:T(8,128)S(1)} %get-tuple-element.13.refs_1_, ...), custom_call_target="tpu_custom_call" | custom-call | tf_op jit(solution)/shard_map/pallas_call | solution.py:687

commit v5 on v4

--- a/solution.py
+++ b/solution.py
@@ -56,9 +56,13 @@
     columns = stacked(np.concatenate([inner] + [left, right] * 4))
     inner_rows = beside(row_table(EDGE + np.arange(ROWS)))
     edge_rows = beside(row_table(np.concatenate([np.arange(EDGE), LX - EDGE + np.arange(EDGE)])))
-    angle = 2.0 * np.pi / LX * np.outer(EDGE + np.arange(ROWS), np.arange(LX))
-    c, s = np.cos(angle), np.sin(angle)
-    rows_back = beside(np.block([[c, -s], [s, c]]))
+    kept = np.arange(ROWS)
+    halves = []
+    for part in (np.concatenate([kept[:EDGE], kept[-EDGE:]]), kept[EDGE:-EDGE]):
+        angle = 2.0 * np.pi / LX * np.outer(EDGE + part, np.arange(LX))
+        c, s = np.cos(angle), np.sin(angle)
+        halves.append(beside(np.block([[c, -s], [s, c]])))
+    rows_back = np.concatenate(halves)
     angle = 2.0 * np.pi / LY * np.outer(np.arange(HALF), EDGE + np.arange(COLUMNS))
     weight = np.where(np.isin(np.arange(HALF), (0, LY // 2)), 1.0, 2.0)[:, None] / (LX * LY)
     back = np.zeros((256, COLUMNS))
@@ -213,27 +217,22 @@
     for k in (4, 3, 2, 1):
         fetches[k].start()
 
-    def pack(source, turn, group):
-        lane = lax.broadcasted_iota(jnp.int32, (ROWS, 128), 1)
-        if group == 0:
-            to_right = jnp.zeros((ROWS, 128), F32)
-            to_left = jnp.zeros((ROWS, 128), F32)
-        else:
-            to_right, to_left = packed[turn, 0], packed[turn, 1]
-        for j in range(4):
-            base = 32 * j
-            low, high = (base, base + EDGE) if group == 0 else (base + EDGE, base)
-            plane = source[4 * group + j]
+    def pack(planes):
+        lane = lax.broadcasted_iota(jnp.int32, planes[0].shape, 1)
+        to_right = jnp.zeros(planes[0].shape, F32)
+        to_left = jnp.zeros(planes[0].shape, F32)
+        for z, plane in enumerate(planes):
+            base = (z % 4) * 32
+            low, high = (base, base + EDGE) if z < 4 else (base + EDGE, base)
             shift = (low - (COLUMNS - EDGE)) % 128
             rolled = pltpu.roll(plane, shift, 1) if shift else plane
             to_right = jnp.where((lane >= low) & (lane < low + EDGE), rolled, to_right)
             rolled = pltpu.roll(plane, high, 1) if high else plane
             to_left = jnp.where((lane >= high) & (lane < high + EDGE), rolled, to_left)
-        packed[turn, 0] = to_right
-        packed[turn, 1] = to_left
+        return to_right, to_left
 
     middle, top, bottom = pl.ds(EDGE, ROWS), pl.ds(0, EDGE), pl.ds(EDGE + ROWS, EDGE)
-    head, tail = pl.ds(0, EDGE), pl.ds(ROWS - EDGE, EDGE)
+    head, tail, trunk = pl.ds(0, EDGE), pl.ds(ROWS - EDGE, EDGE), pl.ds(EDGE, ROWS - 2 * EDGE)
 
     def send(copies):
         for copy, ahead in copies:
@@ -280,23 +279,19 @@
 
         right, left = packed.at[turn, 0], packed.at[turn, 1]
         from_left, from_right = edge_columns.at[turn, 0], edge_columns.at[turn, 1]
-        along = []
-        for group in (0, 1):
-            planes = pl.ds(4 * group, 4)
-            into = edge_rows.at[turn, 0, planes], edge_rows.at[turn, 1, planes]
-            along.append(copy(source.at[planes, tail, :], into[0], 0, 1, 0))
-            along.append(copy(source.at[planes, head, :], into[1], 0, -1, 0))
-        corners = [
+        early = [
+            copy(source.at[:, tail, :], edge_rows.at[turn, 0], 0, 1, 0),
+            copy(source.at[:, head, :], edge_rows.at[turn, 1], 0, -1, 0),
             copy(right.at[tail, :], from_left.at[top, :], 0, 1, 1),
             copy(right.at[head, :], from_left.at[bottom, :], 0, -1, 1),
             copy(left.at[tail, :], from_right.at[top, :], 0, 1, -1),
             copy(left.at[head, :], from_right.at[bottom, :], 0, -1, -1),
         ]
-        across = [
-            copy(right, from_left.at[middle, :], 1, 0, 1),
-            copy(left, from_right.at[middle, :], 1, 0, -1),
-        ]
-        return along, corners, across
+        for rows in (head, tail, trunk):
+            into = pl.ds(rows.start + EDGE, rows.size)
+            early.append(copy(right.at[rows, :], from_left.at[into, :], 1, 0, 1))
+            early.append(copy(left.at[rows, :], from_right.at[into, :], 1, 0, -1))
+        return early[:-2], early[-2:]
 
     def clear_borders():
         rows, columns = jnp.zeros((8, EDGE, 128), F32), jnp.zeros((LX, 128), F32)
@@ -418,20 +413,22 @@
 
         lax.fori_loop(0, LX // 16, blocks, 0)
 
-    def inverse(planes):
+    def inverse(parts):
         rows = []
-        for z in planes[::2]:
+        table = slice(64 * parts[0], 64 * parts[-1] + 64)
+        for z in range(0, 8, 2):
             joint = jnp.concatenate([product_ref[z], product_ref[z + 1]], axis=1)
-            half = dot(wide_ref[0:128, 896:1472], right_triple(joint))
+            half = dot(wide_ref[table, 896:1472], right_triple(joint))
             for b in (0, 1):
                 lanes = slice(128 * b, 128 * b + 128)
-                rows.append(jnp.concatenate([half[:ROWS, lanes], half[ROWS:, lanes]], axis=1))
+                for k in range(len(parts)):
+                    re, im = half[64 * k : 64 * k + 32, lanes], half[64 * k + 32 : 64 * k + 64, lanes]
+                    rows.append(jnp.concatenate([re, im], axis=1))
         full = dot(jnp.concatenate(two(jnp.concatenate(rows, axis=0)), axis=1), tall_ref[768:1280, :])
-        return (full[:, :COLUMNS] + full[:, COLUMNS:]).reshape(len(planes), ROWS, COLUMNS)
-
-    def convolve(turn, mirrored, between):
+        return (full[:, :COLUMNS] + full[:, COLUMNS:]).reshape(8, 32 * len(parts), COLUMNS)
+
+    def convolve(turn, mirrored):
         depth(own_ref, turn, HALO, mirrored, False)
-        between()
         planes = other_ref.at[turn]
         pltpu.make_async_remote_copy(
             src_ref=planes,
@@ -485,32 +482,38 @@
         lax.fori_loop(0, 4, rows, 0)
 
     fetches[0].wait()
-    pack(est_ref, 0, 0)
-    pack(est_ref, 0, 1)
+    packed[0, 0], packed[0, 1] = pack([est_ref[z] for z in range(8)])
     pl.semaphore_wait(barrier, 1 + number(box(1)))
     spread_word(0)
-    along, corners, across = halo_copies(est_ref, 0)
-    send(corners + across + along)
+    early, late = halo_copies(est_ref, 0)
+    send(early + late)
     clear_borders()
     spectrum()
     fetches[1].wait()
     receive_strips(0)
     forward_inner(est_ref, 0)
     receive_edges(0)
-    forward_edge(0)
     hear_word(0)
     spread_word(1)
-    convolve(0, False, lambda: None)
-    late_along, late_corners, late_across = halo_copies(ratio_ref, 1)
-    for group in (0, 1):
-        at = pl.ds(4 * group, 4)
-        ratio_ref[at] = view_ref[at] / inverse(range(4 * group, 4 * group + 4))
-        if group == 1:
-            pack(ratio_ref, 1, 1)
-            send(late_corners + late_across)
-        send(late_along[2 * group : 2 * group + 2])
-        if group == 0:
-            pack(ratio_ref, 1, 0)
+    forward_edge(0)
+    convolve(0, False)
+    early, late = halo_copies(ratio_ref, 1)
+    blurred = inverse((0,))
+    ends = []
+    for rows, at in ((head, slice(0, EDGE)), (tail, slice(EDGE, 2 * EDGE))):
+        ratio = view_ref[:, rows, :] / blurred[:, at]
+        ratio_ref[:, rows, :] = ratio
+        ends.append(ratio)
+    ends = jnp.concatenate(ends, axis=1)
+    for side, strip in enumerate(pack([ends[z] for z in range(8)])):
+        packed[1, side, head, :] = strip[:EDGE]
+        packed[1, side, tail, :] = strip[EDGE:]
+    send(early)
+    ratio = view_ref[:, trunk, :] / inverse((1,))
+    ratio_ref[:, trunk, :] = ratio
+    for side, strip in enumerate(pack([ratio[z] for z in range(8)])):
+        packed[1, side, trunk, :] = strip
+    send(late)
     hear_word(1)
     spread_word(2)
     receive_strips(1)
@@ -519,13 +522,12 @@
     forward_edge(1)
     hear_word(2)
     spread_word(3)
-
-    def tell_partner():
-        hear_word(3)
-        pl.semaphore_signal(pair_sem, inc=1, device_id=device(0, 0, 1), device_id_type=MESH)
-
-    convolve(1, True, tell_partner)
-    updated = est_ref[...] * inverse(range(8))
+    convolve(1, True)
+    hear_word(3)
+    pl.semaphore_signal(pair_sem, inc=1, device_id=device(0, 0, 1), device_id_type=MESH)
+    correction = inverse((0, 1))
+    pieces = [correction[:, :EDGE], correction[:, 2 * EDGE :], correction[:, EDGE : 2 * EDGE]]
+    updated = est_ref[...] * jnp.concatenate(pieces, axis=1)
     column_sums = jnp.sum(updated, axis=0)
     halves = [jnp.sum(column_sums[32 * i : 32 * i + 32], axis=0, keepdims=True) for i in (0, 1)]
     source = lax.broadcasted_iota(jnp.int32, (384, 128), 0) % 128

time: 38.2 us -> 37.5 us (0.982)
  Pallas kernels: 36.8 us -> 36.2 us
    pallas_call x1, Pallas kernels: 36 us -> 35.4 us  [local(): pl.pallas_call(functools.partial(body, nx, ny), out_shape=out_shape, in_s...]
where the time goes in v5:
time: 37.5 us
  Pallas kernels  36.2 us (97%)
  between operations  1.29 us (3%)
    pallas_call x1, Pallas kernels, local(): pl.pallas_call(functools.partial(body, nx, ny), out_shape=out_shape, in_s...  35.4 us
    pallas_call x1, Pallas kernels, local(): pl.pallas_call(hand_over, out_shape=out_shape, in_specs=[vmem] * 6, out_s...  0.78 us

profile of v5, /device:TPU:1, one launch (start us, length us, event | category | flops | bytes accessed | tf_op | source)
XLA Modules:
  0.0 37.5 jit_solution(5462252699942103024)
XLA Ops:
  1.3 35.4 %shard_map.109 = (f32[8,64,128]{2,1,0:T(8,128)S(1)}, f32[4,32,64]{2,1,0:T(8,128)S(1)}, f32[2,16,32]{2,1,0:T(8,128)S(1)}, f32[1,8,16]{2,1,0:T(8,128)S(1)}, f32[1,...) custom-call(s32[1]{0:T(128)S(6)} %copy.12.index_ref, f32[8,64,128]{2,1,0:T(8,128)} %refs_0_.1, f32[8,64,128]{2,1,0:T(8,128)} %refs_1_.1, ...), custom_call_target="tpu_custom_call" | custom-call | tf_op jit(solution)/shard_map/pallas_call | solution.py:643
  36.7 0.8 %shard_map.110 = (f32[8,64,128]{2,1,0:T(8,128)}, f32[4,32,64]{2,1,0:T(8,128)}, f32[2,16,32]{2,1,0:T(8,128)}, f32[1,8,16]{2,1,0:T(8,128)}, f32[1,4,8]{2,1,0:T(4,128)}, /*index=5*/f32[1,32,32]{2,1,0:T(8,128)}) custom-call(f32[8,64,128]{2,1,0:T(8,128)S(1)} %get-tuple-element.12.refs_0_, f32[4,32,64]{2,1,0:T(8,128)S(1)} %get-tuple-element.13.refs_1_, ...), custom_call_target="tpu_custom_call" | custom-call | tf_op jit(solution)/shard_map/pallas_call | solution.py:689

commit v6 on v5

--- a/solution.py
+++ b/solution.py
@@ -311,12 +311,13 @@
                 for turn in (0, 1):
                     edge_columns[turn, side] = columns
 
-    def partner_copy(turn, z):
+    def partner_copy(turn, group):
+        planes = pl.ds(4 * group, 4)
         return pltpu.make_async_remote_copy(
-            src_ref=own_ref.at[turn, z],
-            dst_ref=other_ref.at[turn, z],
+            src_ref=own_ref.at[turn, planes],
+            dst_ref=other_ref.at[turn, planes],
             send_sem=part_send,
-            recv_sem=part_recv.at[turn],
+            recv_sem=part_recv.at[turn, group],
             device_id=device(0, 0, 1),
             device_id_type=MESH,
         )
@@ -335,8 +336,8 @@
             rows.append(jnp.concatenate([plane_of(z), side], axis=1))
         half = dot(left_triple(jnp.concatenate(rows, axis=0)), tall_ref[0:768, :])
         for group in (0, 1):
-            for pair in (0, 1):
-                z = 4 * group + 2 * pair
+            whole = []
+            for z in (4 * group, 4 * group + 2):
                 a = half[z * height : (z + 1) * height]
                 b = half[(z + 1) * height : (z + 2) * height]
                 joint = jnp.concatenate(
@@ -347,13 +348,11 @@
                     axis=0,
                 )
                 full = dot(wide_ref[:, rows_table], right_triple(joint))
-                for b in (0, 1):
-                    part = full[:, 128 * b : 128 * b + 128]
-                    if adding:
-                        own_ref[turn, z + b] = own_ref[turn, z + b] + part
-                        partner_copy(turn, z + b).start()
-                    else:
-                        own_ref[turn, z + b] = part
+                whole += [full[:, :128], full[:, 128:]]
+            for z, part in enumerate(whole, 4 * group):
+                own_ref[turn, z] = own_ref[turn, z] + part if adding else part
+            if adding:
+                partner_copy(turn, group).start()
 
     def forward_inner(source, turn):
         left, right = edge_columns[turn, 0, middle, :], edge_columns[turn, 1, middle, :]
@@ -373,7 +372,7 @@
 
         transform(turn, 2 * EDGE, plane_of, left, right, slice(384, 576), True)
 
-    def depth(x_ref, turn, base, mirrored, adding):
+    def depth(x_ref, turn, base, mirrored, adding, planes):
         def blocks(step, carry):
             block(2 * step)
             block(2 * step + 1)
@@ -382,21 +381,21 @@
         def block(step):
             at = pl.multiple_of(step * 8, 8)
             re, im = pl.ds(at, 8), pl.ds(pl.multiple_of(at + LX, 8), 8)
-            xr = [x_ref[turn, z, re, :] for z in range(8)]
-            xi = [x_ref[turn, z, im, :] for z in range(8)]
+            xr = {z: x_ref[turn, z, re, :] for z in planes}
+            xi = {z: x_ref[turn, z, im, :] for z in planes}
             if adding:
                 yr = [product_ref[z, re, :] for z in range(8)]
                 yi = [product_ref[z, im, :] for z in range(8)]
             else:
                 yr, yi = [None] * 8, [None] * 8
-            xs = [r + i for r, i in zip(xr, xi)]
+            xs = {z: xr[z] + xi[z] for z in planes}
             sums = [[None] * 8 for _ in range(3)]
             for d in range(-7, 8):
                 taps = [kernel_ref[base + d, pl.ds(at + LX * k, 8), :] for k in range(3)]
                 values = (xs, xi, xr) if mirrored else (xs, xr, xi)
                 for out in range(8):
                     z = out + d if mirrored else out - d
-                    if not 0 <= z < 8:
+                    if z not in planes:
                         continue
                     for k in range(3):
                         term = taps[k] * values[k][z]
@@ -428,18 +427,11 @@
         return (full[:, :COLUMNS] + full[:, COLUMNS:]).reshape(8, 32 * len(parts), COLUMNS)
 
     def convolve(turn, mirrored):
-        depth(own_ref, turn, HALO, mirrored, False)
-        planes = other_ref.at[turn]
-        pltpu.make_async_remote_copy(
-            src_ref=planes,
-            dst_ref=planes,
-            send_sem=part_send,
-            recv_sem=part_recv.at[turn],
-            device_id=device(0, 0, 1),
-            device_id_type=MESH,
-        ).wait_recv()
+        depth(own_ref, turn, HALO, mirrored, False, range(8))
         base = HALO + 8 - 16 * gz if mirrored else HALO - 8 + 16 * gz
-        depth(other_ref, turn, base, mirrored, True)
+        for group in (0, 1):
+            partner_copy(turn, group).wait_recv()
+            depth(other_ref, turn, base, mirrored, True, range(4 * group, 4 * group + 4))
 
     def spectrum():
         for k in (4, 3, 2):
@@ -674,7 +666,7 @@
             pltpu.SemaphoreType.DMA((2,)),
             pltpu.SemaphoreType.DMA((2, 2)),
             pltpu.SemaphoreType.DMA,
-            pltpu.SemaphoreType.DMA((2,)),
+            pltpu.SemaphoreType.DMA((2, 2)),
             pltpu.SemaphoreType.DMA,
             pltpu.SemaphoreType.DMA,
             pltpu.SemaphoreType.DMA,

time: 37.5 us -> 36.9 us (0.984)
  Pallas kernels: 36.2 us -> 35.5 us
    pallas_call x1, Pallas kernels: 35.4 us -> 34.7 us  [local(): pl.pallas_call(functools.partial(body, nx, ny), out_shape=out_shape, in_s...]
where the time goes in v6:
time: 36.9 us; the launch traced here: 36.8 us
  Pallas kernels  35.5 us (96%)
  between operations  1.29 us (3%)
    pallas_call x1, Pallas kernels, local(): pl.pallas_call(functools.partial(body, nx, ny), out_shape=out_shape, in_s...  34.7 us
    pallas_call x1, Pallas kernels, local(): pl.pallas_call(hand_over, out_shape=out_shape, in_specs=[vmem] * 6, out_s...  0.78 us

profile of v6, /device:TPU:1, one launch (start us, length us, event | category | flops | bytes accessed | tf_op | source)
XLA Modules:
  0.0 36.8 jit_solution(15475507327197753550)
XLA Ops:
  1.3 34.7 %shard_map.109 = (f32[8,64,128]{2,1,0:T(8,128)S(1)}, f32[4,32,64]{2,1,0:T(8,128)S(1)}, f32[2,16,32]{2,1,0:T(8,128)S(1)}, f32[1,8,16]{2,1,0:T(8,128)S(1)}, f32[1,...) custom-call(s32[1]{0:T(128)S(6)} %copy.12.index_ref, f32[8,64,128]{2,1,0:T(8,128)} %refs_0_.1, f32[8,64,128]{2,1,0:T(8,128)} %refs_1_.1, ...), custom_call_target="tpu_custom_call" | custom-call | tf_op jit(solution)/shard_map/pallas_call | solution.py:635
  36.0 0.8 %shard_map.110 = (f32[8,64,128]{2,1,0:T(8,128)}, f32[4,32,64]{2,1,0:T(8,128)}, f32[2,16,32]{2,1,0:T(8,128)}, f32[1,8,16]{2,1,0:T(8,128)}, f32[1,4,8]{2,1,0:T(4,128)}, /*index=5*/f32[1,32,32]{2,1,0:T(8,128)}) custom-call(f32[8,64,128]{2,1,0:T(8,128)S(1)} %get-tuple-element.12.refs_0_, f32[4,32,64]{2,1,0:T(8,128)S(1)} %get-tuple-element.13.refs_1_, ...), custom_call_target="tpu_custom_call" | custom-call | tf_op jit(solution)/shard_map/pallas_call | solution.py:681

commit v7 on v6

--- a/solution.py
+++ b/solution.py
@@ -530,13 +530,31 @@
     tile_ref[...] = placed[0:1] + pltpu.roll(placed[1:2], 4 * ny, 1)
     me = gz * count + gx * ny + gy
     pl.semaphore_wait(pair_sem, 1)
-    for dx, dy, dz in far:
+    lead = (-gx, -gy, 1 - gz)
+    lead = [jnp.where(d < 0, d + n, d) for d, n in zip(lead, (nx, ny, 2))]
+    opening = far[0]
+    alone = (lead[0] == 0) & (lead[1] == 0) & (lead[2] == 0)
+
+    def wrapped(at, offset, length):
+        moved = at + offset
+        return jnp.where(moved >= length, moved - length, moved)
+
+    for k, offset in enumerate(far):
+        if k == 0:
+            swapped = [jnp.where(alone, o, d) for o, d in zip(opening, lead)]
+        else:
+            same = (lead[0] == offset[0]) & (lead[1] == offset[1]) & (lead[2] == offset[2])
+            swapped = [jnp.where(same, o, d) for o, d in zip(opening, offset)]
         pltpu.make_async_remote_copy(
             src_ref=tile_ref,
             dst_ref=gathered.at[me],
             send_sem=all_send,
             recv_sem=all_recv,
-            device_id=device(dx, dy, dz),
+            device_id={
+                "gx": wrapped(gx, swapped[0], nx),
+                "gy": wrapped(gy, swapped[1], ny),
+                "gz": wrapped(gz, swapped[2], 2),
+            },
             device_id_type=MESH,
         ).start()
     gathered[me] = tile_ref[...]

time: 36.9 us -> 36.7 us (level)
  no operation moved by 1% of the time
where the time goes in v7:
time: 36.7 us; the launch traced here: 36.6 us
  Pallas kernels  35.4 us (96%)
  between operations  1.29 us (4%)
    pallas_call x1, Pallas kernels, local(): pl.pallas_call(functools.partial(body, nx, ny), out_shape=out_shape, in_s...  34.6 us
    pallas_call x1, Pallas kernels, local(): pl.pallas_call(hand_over, out_shape=out_shape, in_specs=[vmem] * 6, out_s...  0.78 us

profile of v7, /device:TPU:1, one launch (start us, length us, event | category | flops | bytes accessed | tf_op | source)
XLA Modules:
  0.0 36.6 jit_solution(2982816860404332021)
XLA Ops:
  1.3 34.6 %shard_map.109 = (f32[8,64,128]{2,1,0:T(8,128)S(1)}, f32[4,32,64]{2,1,0:T(8,128)S(1)}, f32[2,16,32]{2,1,0:T(8,128)S(1)}, f32[1,8,16]{2,1,0:T(8,128)S(1)}, f32[1,...) custom-call(s32[1]{0:T(128)S(6)} %copy.12.index_ref, f32[8,64,128]{2,1,0:T(8,128)} %refs_0_.1, f32[8,64,128]{2,1,0:T(8,128)} %refs_1_.1, ...), custom_call_target="tpu_custom_call" | custom-call | tf_op jit(solution)/shard_map/pallas_call | solution.py:653
  35.9 0.8 %shard_map.110 = (f32[8,64,128]{2,1,0:T(8,128)}, f32[4,32,64]{2,1,0:T(8,128)}, f32[2,16,32]{2,1,0:T(8,128)}, f32[1,8,16]{2,1,0:T(8,128)}, f32[1,4,8]{2,1,0:T(4,128)}, /*index=5*/f32[1,32,32]{2,1,0:T(8,128)}) custom-call(f32[8,64,128]{2,1,0:T(8,128)S(1)} %get-tuple-element.12.refs_0_, f32[4,32,64]{2,1,0:T(8,128)S(1)} %get-tuple-element.13.refs_1_, ...), custom_call_target="tpu_custom_call" | custom-call | tf_op jit(solution)/shard_map/pallas_call | solution.py:699

commit v8 on v6

--- a/solution.py
+++ b/solution.py
@@ -334,7 +334,13 @@
             j = 32 * (z % 4)
             side = jnp.where((lane >= j) & (lane < j + 32), mixed[z // 4], 0.0)
             rows.append(jnp.concatenate([plane_of(z), side], axis=1))
-        half = dot(left_triple(jnp.concatenate(rows, axis=0)), tall_ref[0:768, :])
+        split = 2 if adding else 1
+        size = 8 // split
+        halves = [
+            dot(left_triple(jnp.concatenate(rows[k * size : k * size + size], axis=0)), tall_ref[0:768, :])
+            for k in range(split)
+        ]
+        half = halves[0] if split == 1 else jnp.concatenate(halves, axis=0)
         for group in (0, 1):
             whole = []
             for z in (4 * group, 4 * group + 2):

time: 36.9 us -> 36.6 us (level)
  no operation moved by 1% of the time
where the time goes in v8:
time: 36.6 us; the launch traced here: 36.5 us
  Pallas kernels  35.3 us (96%)
  between operations  1.29 us (4%)
    pallas_call x1, Pallas kernels, local(): pl.pallas_call(functools.partial(body, nx, ny), out_shape=out_shape, in_s...  34.5 us
    pallas_call x1, Pallas kernels, local(): pl.pallas_call(hand_over, out_shape=out_shape, in_specs=[vmem] * 6, out_s...  0.78 us

profile of v8, /device:TPU:1, one launch (start us, length us, event | category | flops | bytes accessed | tf_op | source)
XLA Modules:
  0.0 36.5 jit_solution(16514094073352634263)
XLA Ops:
  1.3 34.5 %shard_map.109 = (f32[8,64,128]{2,1,0:T(8,128)S(1)}, f32[4,32,64]{2,1,0:T(8,128)S(1)}, f32[2,16,32]{2,1,0:T(8,128)S(1)}, f32[1,8,16]{2,1,0:T(8,128)S(1)}, f32[1,...) custom-call(s32[1]{0:T(128)S(6)} %copy.12.index_ref, f32[8,64,128]{2,1,0:T(8,128)} %refs_0_.1, f32[8,64,128]{2,1,0:T(8,128)} %refs_1_.1, ...), custom_call_target="tpu_custom_call" | custom-call | tf_op jit(solution)/shard_map/pallas_call | solution.py:641
  35.8 0.8 %shard_map.110 = (f32[8,64,128]{2,1,0:T(8,128)}, f32[4,32,64]{2,1,0:T(8,128)}, f32[2,16,32]{2,1,0:T(8,128)}, f32[1,8,16]{2,1,0:T(8,128)}, f32[1,4,8]{2,1,0:T(4,128)}, /*index=5*/f32[1,32,32]{2,1,0:T(8,128)}) custom-call(f32[8,64,128]{2,1,0:T(8,128)S(1)} %get-tuple-element.12.refs_0_, f32[4,32,64]{2,1,0:T(8,128)S(1)} %get-tuple-element.13.refs_1_, ...), custom_call_target="tpu_custom_call" | custom-call | tf_op jit(solution)/shard_map/pallas_call | solution.py:687
